TPU v7x, 32 devices: a whole 2x2x4 slice. The times are simulated.
32 devices in a mesh: seq: 16 (over z, y, core), sub: 2 (over x).
Axes of the slice: x: 2, y: 2, z: 4, core: 2. Of those that a mesh axis runs over, the one named last changes fastest.
Arguments:
- tokens: bfloat16 [4096, 1024], P(('seq', 'sub')), may hold values from -6 to 6
- cotangent: bfloat16 [4096, 1024], P(('seq', 'sub')), may hold values from -6 to 6
- fine_qkv: bfloat16 [1024, 3, 1024], replicated, may hold values from -0.1875 to 0.1875
- fine_out: bfloat16 [1024, 1024], replicated, may hold values from -0.1875 to 0.1875
- coarse_qkv: bfloat16 [1024, 3, 1024], P(None, None, 'sub'), may hold values from -0.1875 to 0.1875
- coarse_out: bfloat16 [1024, 1024], P('sub'), may hold values from -0.5 to 0.5
Outputs:
- output: bfloat16 [4096, 1024], P(('seq', 'sub'))
- grad_tokens: bfloat16 [4096, 1024], P(('seq', 'sub'))
All inputs are finite; a program needn't handle non-finite values.
Results may differ from a plain program's by a relative error of at most 0.02.
Values may be sent and summed in bfloat16 or wider, within the bound.
A program may use at most 128 MiB of HBM per device.

v0:
```python
import functools

import jax
import jax.numpy as jnp
from jax import lax
from jax.experimental import pallas as pl
from jax.experimental.pallas import tpu as pltpu
from jax.sharding import PartitionSpec as P

D = 1024
HEADS = 16
HEAD_DIM = 64
WINDOW = 512
POOL = 16
EPS = 1e-06
F32 = jnp.float32
BF16 = jnp.bfloat16
MESH = pl.DeviceIdType.MESH
PAIR = 2 * HEAD_DIM
SCALE = HEAD_DIM ** (-0.5)
VMEM = pl.BlockSpec(memory_space=pltpu.VMEM)
ANY = pl.BlockSpec(memory_space=pl.ANY)
SMEM = pl.BlockSpec(memory_space=pltpu.SMEM)


def dot(a, b):
    return jnp.dot(a, b, preferred_element_type=F32)


def dot_nt(a, b):
    return lax.dot_general(a, b, (((1,), (1,)), ((), ())), preferred_element_type=F32)


def dot_tn(a, b):
    return lax.dot_general(a, b, (((0,), (0,)), ((), ())), preferred_element_type=F32)


def split(x):
    hi = x.astype(BF16)
    return hi, (x - hi.astype(F32)).astype(BF16)


def iota(shape, axis):
    return lax.broadcasted_iota(jnp.int32, shape, axis)


def head_sum(x):
    group = (iota((x.shape[1], 128), 0) // HEAD_DIM == iota((x.shape[1], 128), 1)).astype(F32).astype(BF16)
    hi, lo = split(x)
    return dot(hi, group) + dot(lo, group)


def head_spread(f, width):
    group = (iota((128, width), 1) // HEAD_DIM == iota((128, width), 0)).astype(F32).astype(BF16)
    hi, lo = split(f)
    return dot(hi, group) + dot(lo, group)


def head_rms(raw):
    factor = lax.rsqrt(head_sum(raw * raw) / HEAD_DIM + EPS)
    factor = head_spread(factor, raw.shape[1])
    return raw * factor, factor


def head_back(grad, unit, factor):
    return factor * (grad - unit * head_spread(head_sum(unit * grad) / HEAD_DIM, grad.shape[1]))


def rms_rows(x):
    factor = lax.rsqrt(jnp.mean(x * x, axis=-1, keepdims=True) + EPS)
    return x * factor, factor


def row_back(grad, normed, factor):
    return factor * (grad - normed * jnp.mean(normed * grad, axis=-1, keepdims=True))


def both(pair):
    low = iota(pair.shape, 1) < HEAD_DIM
    wide = pair.astype(F32)
    return jnp.concatenate([jnp.where(low, wide, 0.0), jnp.where(low, 0.0, wide)]).astype(BF16)


def pick(stacked):
    half = stacked.shape[0] // 2
    low = iota((half, PAIR), 1) < HEAD_DIM
    return jnp.where(low, stacked[:half], stacked[half:])


def place():
    subs = lax.axis_size("sub")
    count = lax.axis_size("seq") * subs
    me = lax.axis_index("seq") * subs + lax.axis_index("sub")
    return me, count, subs


def coords(index, subs):
    return (index // subs, index % subs)


def greet_all():
    me, count, subs = place()
    barrier = pltpu.get_barrier_semaphore()

    @pl.loop(1, count)
    def _(k):
        pl.semaphore_signal(
            barrier, inc=1, device_id=coords((me + k) % count, subs), device_id_type=MESH
        )

    pl.semaphore_wait(barrier, count - 1)


def remote(src, dst, send, recv, target, subs):
    return pltpu.make_async_remote_copy(
        src_ref=src, dst_ref=dst, send_sem=send, recv_sem=recv,
        device_id=coords(target, subs), device_id_type=MESH,
    )


class Spread:
    def __init__(self, src, dst, out_sem, mid_sem, last_sem, sent):
        self.me, self.count, self.subs = place()
        self.cores = 2 if lax.axis_size("seq") % 2 == 0 else 1
        self.groups = self.count // self.subs // self.cores
        self.sub = self.me % self.subs
        self.core = self.me // self.subs % self.cores
        self.group = self.me // self.subs // self.cores
        self.src, self.dst, self.sems, self.sent = src, dst, (out_sem, mid_sem, last_sem), sent

    def index(self, k, core, j):
        group = (self.group + self.groups - k) % self.groups
        sub = (self.sub + self.subs - j) % self.subs
        return (group * self.cores + (self.core + core) % self.cores) * self.subs + sub

    def copy(self, phase, j, k):
        if phase == 0:
            spot, source = self.me, self.src
            target, sem = self.index(self.groups - k, 0, 0), self.sems[0].at[k]
        elif phase == 1:
            spot = self.index(k, 0, 0)
            target, sem = self.index(0, 0, self.subs - j), self.sems[1].at[j, k]
        else:
            spot = self.index(k, 0, j)
            target, sem = self.index(0, 1, 0), self.sems[2].at[j, k]
        source = self.src if phase == 0 else self.dst.at[spot]
        return remote(source, self.dst.at[spot], self.sent.at[phase, j, k], sem, target, self.subs)

    def arrive(self, phase, j, k):
        if phase == 0:
            spot, sem = self.index(k, 0, 0), self.sems[0].at[k]
        elif phase == 1:
            spot, sem = self.index(k, 0, j), self.sems[1].at[j, k]
        else:
            spot, sem = self.index(k, 1, j), self.sems[2].at[j, k]
        other = (self.me + 1) % self.count
        return remote(self.dst.at[spot], self.dst.at[spot], self.sent.at[phase, j, k], sem, other, self.subs)

    def relay(self, k):
        for j in range(1, self.subs):
            self.copy(1, j, k).start()
        if self.cores > 1:
            self.copy(2, 0, k).start()

    def start(self):
        self.dst[self.me] = self.src[...]

        @pl.loop(1, self.groups)
        def _(k):
            self.copy(0, 0, k).start()

        self.relay(0)

    def finish(self):
        @pl.loop(1, self.groups)
        def _(k):
            self.arrive(0, 0, k).wait_recv()
            self.relay(k)

        @pl.loop(0, self.groups)
        def _(k):
            for j in range(1, self.subs):
                self.arrive(1, j, k).wait_recv()
                if self.cores > 1:
                    self.copy(2, j, k).start()

        @pl.loop(0, self.groups)
        def _(k):
            for j in range(self.subs):
                if self.cores > 1:
                    self.arrive(2, j, k).wait_recv()
                    self.copy(2, j, k).wait_send()
                if j > 0:
                    self.copy(1, j, k).wait_send()

        @pl.loop(1, self.groups)
        def _(k):
            self.copy(0, 0, k).wait_send()


def spread_sems(count, subs):
    cores = 2 if count // subs % 2 == 0 else 1
    groups = count // subs // cores
    dma = pltpu.SemaphoreType.DMA
    return [dma((groups,)), dma((subs, groups)), dma((subs, groups)), dma((3, subs, groups))]


class Halo:
    def __init__(self, src, dst, sends, recvs, hops, sign):
        self.me, self.count, self.subs = place()
        self.src, self.dst, self.sends, self.recvs = src, dst, sends, recvs
        self.hops, self.sign = hops, sign
        self.paired = lax.axis_size("seq") % 2 == 0
        far_core = self.me // self.subs % 2
        self.first = far_core == (0 if sign > 0 else 1)

    def slot(self, d):
        return self.dst.at[self.hops - d if self.sign > 0 else d - 1]

    def inside(self, index):
        return (index >= 0) & (index < self.count)

    def cuts(self, d):
        if not self.paired or d <= self.subs:
            return self.inside(self.me + self.sign * d)
        target = self.me + self.sign * d + 2 * self.count * self.subs
        core = target // self.subs % 2
        return self.inside(self.me + self.sign * d) & (core == (0 if self.sign > 0 else 1))

    def direct(self, d):
        target = jnp.clip(self.me + self.sign * d, 0, self.count - 1)
        return remote(self.src, self.slot(d), self.sends.at[d - 1], self.recvs.at[d - 1], target, self.subs)

    def passed(self, d):
        target = jnp.clip(self.me + self.sign * self.subs, 0, self.count - 1)
        to = d + self.subs
        return remote(
            self.slot(d), self.slot(to), self.sends.at[self.hops + to - 1], self.recvs.at[to - 1],
            target, self.subs,
        )

    def relays(self, d):
        return self.first & self.inside(self.me - self.sign * d)

    def start(self):
        for d in range(1, self.hops + 1):
            @pl.when(self.cuts(d))
            def _():
                self.direct(d).start()

    def finish(self):
        for d in range(1, self.hops + 1):
            @pl.when(self.inside(self.me - self.sign * d))
            def _():
                self.direct(d).wait_recv()

            if self.paired and d + self.subs <= self.hops:
                @pl.when(self.relays(d))
                def _():
                    self.passed(d).start()

    def drain(self):
        for d in range(1, self.hops + 1):
            @pl.when(self.cuts(d))
            def _():
                self.direct(d).wait_send()

            if self.paired and d + self.subs <= self.hops:
                @pl.when(self.relays(d))
                def _():
                    self.passed(d).wait_send()


class Shift:
    def __init__(self, src, dst, send, recv, distance):
        me, count, subs = place()
        self.me, self.subs, self.target = me, subs, me + distance
        self.args = (src, dst, send, recv)
        self.sends = (me + distance >= 0) & (me + distance < count)
        self.gets = (me - distance >= 0) & (me - distance < count)
        self.copy = remote(src, dst, send, recv, jnp.clip(me + distance, 0, count - 1), subs)

    def start(self):
        @pl.when(self.sends)
        def _():
            self.copy.start()

    def wait(self):
        @pl.when(self.sends)
        def _():
            self.copy.wait_send()

        @pl.when(self.gets)
        def _():
            self.copy.wait_recv()


def comm(body, outs, scratch, ident, specs, *args, out_specs=None):
    return pl.pallas_call(
        body,
        out_shape=outs,
        in_specs=specs,
        out_specs=jax.tree.map(lambda _: ANY, outs) if out_specs is None else out_specs,
        scratch_shapes=scratch,
        compiler_params=pltpu.CompilerParams(
            collective_id=ident, has_side_effects=True, vmem_limit_bytes=60 * 1024 * 1024
        ),
    )(*args)


def local_call(body, outs, *args, smem=True):
    return pl.pallas_call(
        body,
        out_shape=outs,
        in_specs=[SMEM] + [VMEM] * (len(args) - 1),
        out_specs=jax.tree.map(lambda _: VMEM, outs),
        compiler_params=pltpu.CompilerParams(vmem_limit_bytes=60 * 1024 * 1024),
    )(*args)


def second_exchange(hidden_ref, pooled_all, tail, pooled, send, recv, *sems):
    me, count, subs = place()
    rows = hidden_ref.shape[0]
    outs = rows // POOL
    greet_all()
    carry = Shift(hidden_ref.at[pl.ds(rows - POOL, POOL)], tail, send, recv, 1)
    carry.start()
    back = iota((outs, rows), 0) * POOL - iota((outs, rows), 1)
    part = dot(((back >= 0) & (back < POOL)).astype(F32).astype(BF16), hidden_ref[...])
    carry.wait()
    lead = (iota((outs, POOL), 0) == 0) & (iota((outs, POOL), 1) > 0)
    tail_rows = jnp.where(me > 0, tail[...].astype(F32), 0.0).astype(BF16)
    part = part + dot(lead.astype(F32).astype(BF16), tail_rows)
    pooled[...] = (part / POOL).astype(BF16)
    spread = Spread(pooled, pooled_all, *sems)
    spread.start()
    spread.finish()


def third_exchange(far, mixed_all, grad_all, mixed_in, grad_in, sends, recvs, local):
    me, count, subs = place()
    mine = lax.axis_index("sub")
    seq = lax.axis_index("seq")
    outs = mixed_in.shape[1]
    barrier = pltpu.get_barrier_semaphore()
    for k in range(1, subs):
        pl.semaphore_signal(
            barrier, inc=1, device_id=(seq, (mine + k) % subs), device_id_type=MESH
        )
    pl.semaphore_wait(barrier, subs - 1)
    copies = []
    for k in range(1, subs):
        target = seq * subs + (mine + k) % subs
        start = pl.multiple_of(target * outs, outs)
        pieces = (
            (mixed_all.at[pl.ds(start, outs)], mixed_in.at[k]),
            (grad_all.at[pl.ds(start, far)], grad_in.at[k]),
        )
        for which, (src, dst) in enumerate(pieces):
            copies.append(remote(src, dst, sends.at[2 * k + which], recvs.at[2 * k + which], target, subs))
    for copy in copies:
        copy.start()
    start = pl.multiple_of(me * outs, outs)
    own = [
        pltpu.make_async_copy(mixed_all.at[pl.ds(start, outs)], mixed_in.at[0], local.at[0]),
        pltpu.make_async_copy(grad_all.at[pl.ds(start, far)], grad_in.at[0], local.at[1]),
    ]
    for copy in own:
        copy.start()
    for copy in copies + own:
        copy.wait()


def fourth_exchange(hops, stats_ref, after, sends, recvs):
    me, count, subs = place()
    barrier = pltpu.get_barrier_semaphore()
    for d in range(1, hops + 1):
        for other in (me - d, me + d):

            @pl.when((other >= 0) & (other < count))
            def _():
                pl.semaphore_signal(
                    barrier, inc=1, device_id=coords(jnp.clip(other, 0, count - 1), subs),
                    device_id_type=MESH,
                )

    pl.semaphore_wait(barrier, jnp.minimum(me, hops) + jnp.minimum(count - 1 - me, hops))

    moves = [
        Shift(stats_ref, after.at[d - 1], sends.at[d - 1], recvs.at[d - 1], -d)
        for d in range(1, hops + 1)
    ]
    for move in moves:
        move.start()
    for move in moves:
        move.wait()


def window_mask(rows, keys, anchor):
    gap = keys - rows + iota((rows, keys), 0) - iota((rows, keys), 1)
    return (gap >= 0) & (gap < WINDOW) & (anchor - (keys - rows) + iota((rows, keys), 1) >= 0)


def fine_forward(
    hops, x_ref, cot_ref, cg_ref, w_hbm, out_hbm,
    q_all, k_all, v_all, unit_q, unit_k, scale_q, scale_k, tot_ref, att_ref, hidden_ref, cg_all,
    after, cot_after,
    before, w_ref, out_w, load, sends, recvs, *sems,
):
    me, count, subs = place()
    rows = x_ref.shape[0]
    margin = hops * rows
    anchor = me * rows
    loads = [
        pltpu.make_async_copy(w_hbm, w_ref, load.at[0]),
        pltpu.make_async_copy(out_hbm, out_w, load.at[1]),
    ]
    for one in loads:
        one.start()
    greet_all()
    down = Halo(x_ref, before, sends.at[0], recvs.at[0], hops, 1)
    up = Halo(x_ref, after, sends.at[1], recvs.at[1], hops, -1)
    up_cot = Halo(cot_ref, cot_after, sends.at[2], recvs.at[2], hops, -1)
    spread = Spread(cg_ref, cg_all, *sems)
    down.start()
    spread.start()
    own = x_ref[...].astype(F32)
    own_b = rms_rows(own)[0].astype(BF16)
    loads[0].wait()
    unit, factor = head_rms(dot(own_b, w_ref[0]))
    q_all[...] = unit.astype(BF16)
    unit_q[...] = unit
    scale_q[...] = factor
    unit, factor = head_rms(dot(own_b, w_ref[1]))
    k_all[pl.ds(margin, rows), :] = unit.astype(BF16)
    unit_k[...] = unit
    scale_k[...] = factor
    v_all[pl.ds(margin, rows), :] = dot(own_b, w_ref[2]).astype(BF16)
    down.finish()
    up.start()
    up_cot.start()
    prev = before[...].reshape(margin, D).astype(F32)
    prev = jnp.where(anchor - margin + iota(prev.shape, 0) >= 0, prev, 0.0)
    prev_b = rms_rows(prev)[0].astype(BF16)
    k_all[pl.ds(0, margin), :] = head_rms(dot(prev_b, w_ref[1]))[0].astype(BF16)
    v_all[pl.ds(0, margin), :] = dot(prev_b, w_ref[2]).astype(BF16)
    mask = window_mask(rows, margin + rows, anchor)
    mask = jnp.concatenate([mask.astype(F32)] * 2) > 0
    lane = iota((rows, 128), 1)
    totals = jnp.ones((rows, 128), F32)
    for p in range(HEADS // 2):
        cols = pl.ds(p * PAIR, PAIR)
        s = dot_nt(both(q_all[pl.ds(0, rows), cols]), k_all[:, cols]) * SCALE
        e = jnp.where(mask, jnp.exp(s), 0.0)
        t = jnp.sum(e, axis=-1, keepdims=True)
        prob = (e * (1.0 / t)).astype(BF16)
        att_ref[:, cols] = pick(dot(prob, v_all[:, cols])).astype(BF16)
        totals = jnp.where(lane == 2 * p, t[:rows], totals)
        totals = jnp.where(lane == 2 * p + 1, t[rows:], totals)
    tot_ref[...] = totals
    loads[1].wait()
    hidden_ref[...] = (own + dot(att_ref[...], out_w[...])).astype(BF16)
    up.finish()
    up_cot.finish()
    spread.finish()
    down.drain()
    up.drain()
    up_cot.drain()


def coarse_level(pos, pooled_ref, cg_ref, w_ref, out_w, mixed_ref, grad_ref):
    count, width = pooled_ref.shape[0], w_ref.shape[2]
    normed_b = rms_rows(pooled_ref[...].astype(F32))[0].astype(BF16)
    uq, fq = head_rms(dot(normed_b, w_ref[0]))
    uk, fk = head_rms(dot(normed_b, w_ref[1]))
    qb, kb = uq.astype(BF16), uk.astype(BF16)
    vb = dot(normed_b, w_ref[2]).astype(BF16)
    gb = dot_nt(cg_ref[...], out_w[...]).astype(BF16)
    block = min(count, 256)
    att_p, dq_p, dk_p, dv_p = [], [], [], []
    for p in range(width // PAIR):
        cols = slice(p * PAIR, (p + 1) * PAIR)
        att_b, dq_b, dk, dv = [], [], None, None
        kp, vp = kb[:, cols], vb[:, cols]
        for b in range(count // block):
            rows = slice(b * block, (b + 1) * block)
            qs, gs = both(qb[rows, cols]), both(gb[rows, cols])
            s = dot_nt(qs, kp) * SCALE
            where = iota((2 * block, count), 0) % block + b * block >= iota((2 * block, count), 1)
            e = jnp.where(where, jnp.exp(s), 0.0)
            full = e * (1.0 / jnp.sum(e, axis=-1, keepdims=True))
            prob = full.astype(BF16)
            att = pick(dot(prob, vp)).astype(BF16)
            att_b.append(att)
            att2 = jnp.concatenate([att.astype(F32)] * 2)
            delta = jnp.sum(gs.astype(F32) * att2, axis=-1, keepdims=True)
            ds = (full * (dot_nt(gs, vp) - delta)).astype(BF16)
            dq_b.append(pick(dot(ds, kp)) * SCALE)
            dk_t, dv_t = dot_tn(ds, qs) * SCALE, dot_tn(prob, gs)
            dk = dk_t if dk is None else dk + dk_t
            dv = dv_t if dv is None else dv + dv_t
        att_p.append(jnp.concatenate(att_b))
        dq_p.append(jnp.concatenate(dq_b))
        dk_p.append(dk)
        dv_p.append(dv)
    join = lambda parts: jnp.concatenate(parts, axis=1)
    mixed_ref[...] = dot(join(att_p), out_w[...]).astype(BF16)
    dq = head_back(join(dq_p), uq, fq).astype(BF16)
    dk = head_back(join(dk_p), uk, fk).astype(BF16)
    dv = join(dv_p).astype(BF16)
    total = dot_nt(dq, w_ref[0]) + dot_nt(dk, w_ref[1]) + dot_nt(dv, w_ref[2])
    grad_ref[pl.ds(0, count), :] = total.astype(BF16)
    extra = grad_ref.shape[0] - count
    grad_ref[pl.ds(count, extra), :] = jnp.zeros((extra, D), BF16)


def middle(
    pos, hidden_ref, mixed_in, grad_in, pooled_ref, cg_ref, cot_ref, cot_after, att_ref, tot_ref, out_w,
    output_ref, hg_ref, g_all, delta_ref, stats_ref,
):
    rows = hidden_ref.shape[0]
    outs = rows // POOL
    ahead = cot_after.shape[0]
    far = grad_in.shape[1]
    start = pos[0] * rows
    pooled = pooled_ref[...].astype(F32)
    mixed = jnp.sum(mixed_in[...].astype(F32), axis=0)
    state = (pooled[:outs] + mixed).astype(BF16)
    onto = (iota((rows, outs), 0) // POOL == iota((rows, outs), 1)).astype(F32).astype(BF16)
    output_ref[...] = (hidden_ref[...].astype(F32) + dot(onto, state)).astype(BF16)
    nxt = cot_after[...].astype(F32)
    nxt = jnp.where(start + rows + iota(nxt.shape, 0) < pos[1] * rows, nxt, 0.0)
    cot = jnp.concatenate([cot_ref[...].astype(F32), nxt])
    length = rows + ahead
    near = length // POOL
    groups = (iota((near, length), 1) // POOL == iota((near, length), 0)).astype(F32).astype(BF16)
    cg = jnp.concatenate([dot(groups, cot.astype(BF16)), cg_ref[...].astype(F32)[near:]])
    ng = jnp.sum(grad_in[...].astype(F32), axis=0)
    normed, factor = rms_rows(pooled)
    pg = (cg + row_back(ng, normed, factor)) / POOL
    pg = jnp.where(pos[0] * outs + iota(pg.shape, 0) < pos[1] * outs, pg, 0.0)
    lift = ((iota((length, far), 0) + POOL - 1) // POOL == iota((length, far), 1)).astype(F32).astype(BF16)
    hi, lo = split(pg)
    hidden_grad = cot + dot(lift, hi) + dot(lift, lo)
    hg_ref[...] = hidden_grad[:rows]
    g_all[...] = dot_nt(hidden_grad.astype(BF16), out_w[...]).astype(BF16)
    delta = head_sum(g_all[pl.ds(0, rows), :].astype(F32) * att_ref[...].astype(F32))
    delta_ref[...] = delta
    stats_ref[pl.ds(0, HEADS), :] = tot_ref[...].T[:HEADS]
    stats_ref[pl.ds(HEADS, HEADS), :] = delta.T[:HEADS]


def fine_backward(
    pos, x_ref, next_ref, w_ref, q_own, k_all, v_all, g_all, own_stats, after, tot_ref, delta_ref,
    unit_q, unit_k, scale_q, scale_k, hg_ref, grad_ref,
):
    rows = x_ref.shape[0]
    hops = after.shape[0]
    margin = k_all.shape[0] - rows
    length = g_all.shape[0]
    anchor = pos[0] * rows
    nxt = next_ref[...].astype(F32)
    nxt = jnp.where(anchor + rows + iota(nxt.shape, 0) < pos[1] * rows, nxt, 0.0)
    q_next = head_rms(dot(rms_rows(nxt)[0].astype(BF16), w_ref[0]))[0].astype(BF16)
    q_all = jnp.concatenate([q_own[...], q_next])
    mask = window_mask(rows, margin + rows, anchor)
    mask = jnp.concatenate([mask.astype(F32)] * 2) > 0
    gap = iota((rows, length), 1) - iota((rows, length), 0)
    mask_t = (gap >= 0) & (gap < WINDOW) & (anchor + iota((rows, length), 1) < pos[1] * rows)
    stats = jnp.concatenate([own_stats[...]] + [after[d] for d in range(hops)], axis=1)
    stats = jnp.where(anchor + iota(stats.shape, 1) < pos[1] * rows, stats, 1.0)
    totals, deltas = tot_ref[...], delta_ref[...]
    dq_p, dk_p, dv_p = [], [], []
    for p in range(HEADS // 2):
        cols = pl.ds(p * PAIR, PAIR)
        kp, vp, gp = k_all[:, cols], v_all[:, cols], g_all[:, cols]
        qp = q_all[:, p * PAIR : (p + 1) * PAIR]
        s = dot_nt(both(qp[:rows]), kp) * SCALE
        e = jnp.where(mask, jnp.exp(s), 0.0)
        column = lambda m: jnp.concatenate([m[:, 2 * p : 2 * p + 1], m[:, 2 * p + 1 : 2 * p + 2]])
        ds = e * (1.0 / column(totals)) * (dot_nt(both(gp[:rows]), vp) - column(deltas))
        dq_p.append(pick(dot(ds.astype(BF16), kp)) * SCALE)
        k_own, v_own = kp[margin:], vp[margin:]
        qs, gs = both(qp), both(gp)
        dk = dv = jnp.zeros((rows, PAIR), F32)
        for h in range(2):
            part = slice(h * length, (h + 1) * length)
            st = dot_nt(k_own, qs[part]) * SCALE
            head = 2 * p + h
            pt = jnp.where(mask_t, jnp.exp(st), 0.0) * (1.0 / stats[head : head + 1])
            dst = pt * (dot_nt(v_own, gs[part]) - stats[HEADS + head : HEADS + head + 1])
            dk = dk + dot(dst.astype(BF16), qs[part])
            dv = dv + dot(pt.astype(BF16), gs[part])
        dk_p.append(dk * SCALE)
        dv_p.append(dv)
    join = lambda parts: jnp.concatenate(parts, axis=1)
    dq = head_back(join(dq_p), unit_q[...], scale_q[...]).astype(BF16)
    dk = head_back(join(dk_p), unit_k[...], scale_k[...]).astype(BF16)
    dv = join(dv_p).astype(BF16)
    total = dot_nt(dq, w_ref[0]) + dot_nt(dk, w_ref[1]) + dot_nt(dv, w_ref[2])
    normed, factor = rms_rows(x_ref[...].astype(F32))
    grad_ref[...] = (hg_ref[...] + row_back(total, normed, factor)).astype(BF16)


def per_device(tokens, cotangent, fine_qkv, fine_out, coarse_qkv, coarse_out):
    rows = tokens.shape[0]
    hops = -(-WINDOW // rows)
    outs = rows // POOL
    me, count, subs = place()
    pos = jnp.stack([me, jnp.int32(count)]).astype(jnp.int32)
    far = (hops + 2) * outs
    shape = jax.ShapeDtypeStruct
    dma = pltpu.SemaphoreType.DMA
    fine_w = jnp.transpose(fine_qkv, (1, 0, 2))
    coarse_w = jnp.transpose(coarse_qkv, (1, 0, 2))
    coarse_grad = cotangent.astype(F32).reshape(outs, POOL, D).sum(axis=1).astype(BF16)
    length = (hops + 1) * rows
    flat = lambda a: a.reshape(-1, D)
    q_own, k_all, v_all, unit_q, unit_k, scale_q, scale_k, totals, attended, hidden, cg_all, after, cot_after = comm(
        functools.partial(fine_forward, hops),
        [shape((rows, D), BF16)] + [shape((length, D), BF16)] * 2 + [shape((rows, D), F32)] * 4
        + [shape((rows, 128), F32)] + [shape((rows, D), BF16)] * 2
        + [shape((count, outs, D), BF16)] + [shape((hops, rows, D), BF16)] * 2,
        [pltpu.VMEM((hops, rows, D), BF16), pltpu.VMEM(fine_w.shape, BF16), pltpu.VMEM(fine_out.shape, BF16),
         dma((2,)), dma((3, 2 * hops)), dma((3, hops))] + spread_sems(count, subs),
        0, [VMEM] * 3 + [ANY] * 2, tokens, cotangent, coarse_grad, fine_w, fine_out,
        out_specs=[VMEM] * 13,
    )
    pooled_all = comm(
        second_exchange,
        shape((count, outs, D), BF16),
        [pltpu.VMEM((POOL, D), BF16), pltpu.VMEM((outs, D), BF16), dma, dma] + spread_sems(count, subs),
        1, [VMEM], hidden, out_specs=VMEM,
    )
    pooled_all, cg_all = flat(pooled_all), flat(cg_all)
    mixed_all, grad_all = local_call(
        coarse_level,
        [shape((count * outs, D), BF16), shape((count * outs + far, D), BF16)],
        pos, pooled_all, cg_all, coarse_w, coarse_out,
    )
    mixed_in, grad_in = comm(
        functools.partial(third_exchange, far),
        (shape((subs, outs, D), BF16), shape((subs, far, D), BF16)),
        [dma((2 * subs,)), dma((2 * subs,)), dma((2,))],
        2, [VMEM, VMEM], mixed_all, grad_all,
    )
    tail = lambda a: lax.dynamic_slice_in_dim(jnp.pad(a, ((0, far), (0, 0))), me * outs, far)
    output, hidden_grad, g_all, delta, stats = local_call(
        middle,
        [shape((rows, D), BF16), shape((rows, D), F32), shape((length, D), BF16),
         shape((rows, 128), F32), shape((2 * HEADS, rows), F32)],
        pos, hidden, mixed_in, grad_in, tail(pooled_all), tail(cg_all), cotangent, flat(cot_after),
        attended, totals, fine_out,
    )
    stats_after = comm(
        functools.partial(fourth_exchange, hops),
        shape((hops, 2 * HEADS, rows), F32),
        [dma((hops,)), dma((hops,))],
        3, [VMEM], stats,
    )
    grad_tokens = local_call(
        fine_backward, shape((rows, D), BF16),
        pos, tokens, flat(after), fine_w, q_own, k_all, v_all, g_all, stats, stats_after, totals, delta,
        unit_q, unit_k, scale_q, scale_k, hidden_grad,
    )
    return (output, grad_tokens)


def solution(mesh):
    placed = (
        P(("seq", "sub"), None),
        P(("seq", "sub"), None),
        P(),
        P(),
        P(None, None, "sub"),
        P("sub", None),
    )
    return jax.shard_map(
        per_device,
        mesh=mesh,
        in_specs=placed,
        out_specs=(P(("seq", "sub"), None), P(("seq", "sub"), None)),
        check_vma=False,
    )
```

profile of v0, /device:TPU:3, one launch (start us, length us, event | category | flops | bytes accessed | tf_op | source)
XLA Modules:
  0.0 129.7 jit_solution(13834113394579032714)
XLA Ops:
  0.6 0.6 pad_add_fusion.pos
  1.3 1.7 %bitcast_reduce_fusion.cg_ref = bf16[8,1024]{1,0:T(8,128)(2,1)} fusion(bf16[128,1024]{1,0:T(8,128)(2,1)} %cot_ref.3), kind=kLoop, calls=%fused_computation.2 | loop fusion | flops 122880 | bytes 278528 | tf_op jit(solution)/shard_map/reduce_sum | solution.py:616
  2.9 50.6 %shard_map.77 = (bf16[128,1024]{1,0:T(8,128)(2,1)}, bf16[640,1024]{1,0:T(8,128)(2,1)}, bf16[640,1024]{1,0:T(8,128)(2,1)}, f32[128,1024]{1,0:T(8,128)}, f32[128,1...) custom-call(bf16[128,1024]{1,0:T(8,128)(2,1)} %x_ref.3, ...), custom_call_target="tpu_custom_call" | custom-call | tf_op jit(solution)/shard_map/pallas_call | solution.py:299
  53.6 27.1 %shard_map.78 = bf16[32,8,1024]{2,1,0:T(8,128)(2,1)} custom-call(bf16[128,1024]{1,0:T(8,128)(2,1)} %get-tuple-element.24.hidden_ref), custom_call_target="tpu_custom_call" | custom-call | tf_op jit(solution)/shard_map/pallas_call | solution.py:299
  80.7 1.7 %pad_dynamic-slice_fusion = (bf16[48,1024]{1,0:T(8,128)(2,1)}, bf16[48,1024]{1,0:T(8,128)(2,1)}) fusion(s32[]{:T(128)S(6)} %select_n.4, bf16[256,1024]{1,0:T(8,128)(2,1)} %bitcast.14, bf16[256,1024]{1,0:T(8,128)(2,1)} %bitcast.11), kind=kLoop, calls=%fused_computation | loop fusion | bytes 1245188 | tf_op jit(solution)/shard_map/dynamic_slice | solution.py:647
  82.4 10.5 %shard_map.79 = (bf16[256,1024]{1,0:T(8,128)(2,1)}, bf16[304,1024]{1,0:T(8,128)(2,1)}) custom-call(s32[2]{0:T(128)} %pad_add_fusion.pos, bf16[256,1024]{1,0:T(8,128)(2,1)} %bitcast.12, bf16[256,1024]{1,0:T(8,128)(2,1)} %bitcast.15, bf16[3,1024,512]{2,1,0:T(8,128)(2,1)} %bitcast.13, bf16[512,1024]{1,0:T(8,128)(2,1)} %out_w.2), custom_call_target="tpu_custom_call" | custom-call | tf_op jit(solution)/shard_map/pallas_call | solution.py:312
  92.9 6.0 %shard_map.80 = (bf16[2,8,1024]{2,1,0:T(8,128)(2,1)}, bf16[2,48,1024]{2,1,0:T(8,128)(2,1)}) custom-call(bf16[256,1024]{1,0:T(8,128)(2,1)} %get-tuple-element.26.mixed_all, bf16[304,1024]{1,0:T(8,128)(2,1)} %get-tuple-element.27.grad_all), custom_call_target="tpu_custom_call" | custom-call | tf_op jit(solution)/shard_map/pallas_call | solution.py:299
  98.9 6.0 %shard_map.81 = (bf16[128,1024]{1,0:T(8,128)(2,1)}, f32[128,1024]{1,0:T(8,128)}, bf16[640,1024]{1,0:T(8,128)(2,1)}, f32[128,128]{1,0:T(8,128)}, f32[32,128]{1,0:T(8,128)}) custom-call(s32[2]{0:T(128)} %pad_add_fusion.pos, bf16[128,1024]{1,0:T(8,128)(2,1)} %get-tuple-element.24.hidden_ref, bf16[2,8,1024]{2,1,0:T(8,128)(2,1)} %get-tuple-element.28.mixed_in, ...), custom_call_target="tpu_custom_call" | custom-call | tf_op jit(solution)/shard_map/pallas_call | solution.py:312
  104.9 5.8 %shard_map.82.after = f32[4,32,128]{2,1,0:T(8,128)} custom-call(f32[32,128]{1,0:T(8,128)} %get-tuple-element.39.stats_ref.own_stats), custom_call_target="tpu_custom_call" | custom-call | tf_op jit(solution)/shard_map/pallas_call | solution.py:299
  110.7 18.9 %shard_map.83 = bf16[128,1024]{1,0:T(8,128)(2,1)} custom-call(s32[2]{0:T(128)} %pad_add_fusion.pos, bf16[128,1024]{1,0:T(8,128)(2,1)} %x_ref.3, bf16[512,1024]{1,0:T(8,128)(2,1)} %bitcast.16, bf16[3,1024,1024]{2,1,0:T(8,128)(2,1)} %bitcast.10, bf16[128,1024]{1,0:T(8,128)(2,1)} %get-tuple-element.35.q_own, bf16[640,1024]{1,0:T(8,128)(2,1)} %get-tuple-element.36.k_all, ...), custom_call_target="tpu_custom_call" | custom-call | tf_op jit(solution)/shard_map/pallas_call | solution.py:312
where the time goes:
time: 132 us; the launch traced here: 130 us
  Pallas kernels  125 us (95%)
  other arithmetic  2.3 us (2%)
  local copies, waits for them, and re-layouts  1.66 us (1%)
    pallas_call x4, Pallas kernels, comm(): pl.pallas_call(body, out_shape=outs, in_specs=specs, out_specs=jax.tree.m...  89.6 us
    pallas_call x3, Pallas kernels, local_call(): pl.pallas_call(body, out_shape=outs, in_specs=[SMEM] + [VMEM] * (len(args...  35.4 us

commit v1 on v0

v1 whole, which is shorter than its diff:
```python
import functools
import math

import jax
import jax.numpy as jnp
from jax import lax
from jax.experimental import pallas as pl
from jax.experimental.pallas import tpu as pltpu
from jax.sharding import PartitionSpec as P

D = 1024
HEADS = 16
HEAD_DIM = 64
WINDOW = 512
POOL = 16
EPS = 1e-06
F32 = jnp.float32
BF16 = jnp.bfloat16
MESH = pl.DeviceIdType.MESH
PAIR = 2 * HEAD_DIM
SCALE = HEAD_DIM ** (-0.5)
LN2 = math.log(2.0)
QUERY = SCALE / LN2
VMEM = pl.BlockSpec(memory_space=pltpu.VMEM)
ANY = pl.BlockSpec(memory_space=pl.ANY)
SMEM = pl.BlockSpec(memory_space=pltpu.SMEM)


def dot(a, b):
    return jnp.dot(a, b, preferred_element_type=F32)


def dot_nt(a, b):
    return lax.dot_general(a, b, (((1,), (1,)), ((), ())), preferred_element_type=F32)


def dot_tn(a, b):
    return lax.dot_general(a, b, (((0,), (0,)), ((), ())), preferred_element_type=F32)


def split(x):
    hi = x.astype(BF16)
    return hi, (x - hi.astype(F32)).astype(BF16)


def iota(shape, axis):
    return lax.broadcasted_iota(jnp.int32, shape, axis)


def head_sum(x):
    group = (iota((x.shape[1], 128), 0) // HEAD_DIM == iota((x.shape[1], 128), 1)).astype(F32).astype(BF16)
    hi, lo = split(x)
    return dot(hi, group) + dot(lo, group)


def head_mean(x):
    group = iota((PAIR, PAIR), 0) // HEAD_DIM == iota((PAIR, PAIR), 1) // HEAD_DIM
    group = jnp.where(group, 1.0 / HEAD_DIM, 0.0).astype(BF16)
    x = x.astype(BF16)
    return jnp.concatenate([dot(x[:, c : c + PAIR], group) for c in range(0, x.shape[1], PAIR)], axis=1)


def head_rms(raw):
    factor = lax.rsqrt(head_mean(raw * raw) + EPS)
    return raw * factor, factor


def head_back(grad, unit, factor):
    return factor * (grad - unit * head_mean(unit * grad))


def rms_rows(x):
    factor = lax.rsqrt(jnp.mean(x * x, axis=-1, keepdims=True) + EPS)
    return x * factor, factor


def row_back(grad, normed, factor):
    return factor * (grad - normed * jnp.mean(normed * grad, axis=-1, keepdims=True))


def both(pair):
    low = iota(pair.shape, 1) < HEAD_DIM
    wide = pair.astype(F32)
    return jnp.concatenate([jnp.where(low, wide, 0.0), jnp.where(low, 0.0, wide)]).astype(BF16)


def pick(stacked):
    half = stacked.shape[0] // 2
    low = iota((half, PAIR), 1) < HEAD_DIM
    return jnp.where(low, stacked[:half], stacked[half:])


def place():
    subs = lax.axis_size("sub")
    count = lax.axis_size("seq") * subs
    me = lax.axis_index("seq") * subs + lax.axis_index("sub")
    return me, count, subs


def coords(index, subs):
    return (index // subs, index % subs)


def greet_all():
    me, count, subs = place()
    barrier = pltpu.get_barrier_semaphore()

    @pl.loop(1, count)
    def _(k):
        pl.semaphore_signal(
            barrier, inc=1, device_id=coords((me + k) % count, subs), device_id_type=MESH
        )


def met_all():
    pl.semaphore_wait(pltpu.get_barrier_semaphore(), lax.axis_size("seq") * lax.axis_size("sub") - 1)


def remote(src, dst, send, recv, target, subs):
    return pltpu.make_async_remote_copy(
        src_ref=src, dst_ref=dst, send_sem=send, recv_sem=recv,
        device_id=coords(target, subs), device_id_type=MESH,
    )


class Spread:
    def __init__(self, src, dst, out_sem, mid_sem, last_sem, sent):
        self.me, self.count, self.subs = place()
        self.cores = 2 if lax.axis_size("seq") % 2 == 0 else 1
        self.groups = self.count // self.subs // self.cores
        self.sub = self.me % self.subs
        self.core = self.me // self.subs % self.cores
        self.group = self.me // self.subs // self.cores
        self.src, self.dst, self.sems, self.sent = src, dst, (out_sem, mid_sem, last_sem), sent

    def index(self, k, core, j):
        group = (self.group + self.groups - k) % self.groups
        sub = (self.sub + self.subs - j) % self.subs
        return (group * self.cores + (self.core + core) % self.cores) * self.subs + sub

    def copy(self, phase, j, k):
        if phase == 0:
            spot, source = self.me, self.src
            target, sem = self.index(self.groups - k, 0, 0), self.sems[0].at[k]
        elif phase == 1:
            spot = self.index(k, 0, 0)
            target, sem = self.index(0, 0, self.subs - j), self.sems[1].at[j, k]
        else:
            spot = self.index(k, 0, j)
            target, sem = self.index(0, 1, 0), self.sems[2].at[j, k]
        source = self.src if phase == 0 else self.dst.at[spot]
        return remote(source, self.dst.at[spot], self.sent.at[phase, j, k], sem, target, self.subs)

    def arrive(self, phase, j, k):
        if phase == 0:
            spot, sem = self.index(k, 0, 0), self.sems[0].at[k]
        elif phase == 1:
            spot, sem = self.index(k, 0, j), self.sems[1].at[j, k]
        else:
            spot, sem = self.index(k, 1, j), self.sems[2].at[j, k]
        other = (self.me + 1) % self.count
        return remote(self.dst.at[spot], self.dst.at[spot], self.sent.at[phase, j, k], sem, other, self.subs)

    def relay(self, k):
        for j in range(1, self.subs):
            self.copy(1, j, k).start()
        if self.cores > 1:
            self.copy(2, 0, k).start()

    def start(self):
        self.dst[self.me] = self.src[...]

        @pl.loop(1, self.groups)
        def _(k):
            self.copy(0, 0, k).start()

        self.relay(0)

    def finish(self):
        @pl.loop(1, self.groups)
        def _(k):
            self.arrive(0, 0, k).wait_recv()
            self.relay(k)

        @pl.loop(0, self.groups)
        def _(k):
            for j in range(1, self.subs):
                self.arrive(1, j, k).wait_recv()
                if self.cores > 1:
                    self.copy(2, j, k).start()

        @pl.loop(0, self.groups)
        def _(k):
            for j in range(self.subs):
                if self.cores > 1:
                    self.arrive(2, j, k).wait_recv()
                    self.copy(2, j, k).wait_send()
                if j > 0:
                    self.copy(1, j, k).wait_send()

        @pl.loop(1, self.groups)
        def _(k):
            self.copy(0, 0, k).wait_send()


def spread_sems(count, subs):
    cores = 2 if count // subs % 2 == 0 else 1
    groups = count // subs // cores
    dma = pltpu.SemaphoreType.DMA
    return [dma((groups,)), dma((subs, groups)), dma((subs, groups)), dma((3, subs, groups))]


class Halo:
    def __init__(self, src, dst, sends, recvs, hops, sign):
        self.me, self.count, self.subs = place()
        self.src, self.dst, self.sends, self.recvs = src, dst, sends, recvs
        self.hops, self.sign = hops, sign
        self.paired = lax.axis_size("seq") % 2 == 0
        far_core = self.me // self.subs % 2
        self.first = far_core == (0 if sign > 0 else 1)

    def slot(self, d):
        return self.dst.at[self.hops - d if self.sign > 0 else d - 1]

    def inside(self, index):
        return (index >= 0) & (index < self.count)

    def cuts(self, d):
        if not self.paired or d <= self.subs:
            return self.inside(self.me + self.sign * d)
        target = self.me + self.sign * d + 2 * self.count * self.subs
        core = target // self.subs % 2
        return self.inside(self.me + self.sign * d) & (core == (0 if self.sign > 0 else 1))

    def direct(self, d):
        target = jnp.clip(self.me + self.sign * d, 0, self.count - 1)
        return remote(self.src, self.slot(d), self.sends.at[d - 1], self.recvs.at[d - 1], target, self.subs)

    def passed(self, d):
        target = jnp.clip(self.me + self.sign * self.subs, 0, self.count - 1)
        to = d + self.subs
        return remote(
            self.slot(d), self.slot(to), self.sends.at[self.hops + to - 1], self.recvs.at[to - 1],
            target, self.subs,
        )

    def relays(self, d):
        return self.first & self.inside(self.me - self.sign * d)

    def start(self):
        for d in range(1, self.hops + 1):
            @pl.when(self.cuts(d))
            def _():
                self.direct(d).start()

    def land(self, d):
        @pl.when(self.inside(self.me - self.sign * d))
        def _():
            self.direct(d).wait_recv()

        if self.paired and d + self.subs <= self.hops:
            @pl.when(self.relays(d))
            def _():
                self.passed(d).start()

    def finish(self):
        for d in range(1, self.hops + 1):
            self.land(d)

    def drain(self):
        for d in range(1, self.hops + 1):
            @pl.when(self.cuts(d))
            def _():
                self.direct(d).wait_send()

            if self.paired and d + self.subs <= self.hops:
                @pl.when(self.relays(d))
                def _():
                    self.passed(d).wait_send()


class Shift:
    def __init__(self, src, dst, send, recv, distance):
        me, count, subs = place()
        self.me, self.subs, self.target = me, subs, me + distance
        self.args = (src, dst, send, recv)
        self.sends = (me + distance >= 0) & (me + distance < count)
        self.gets = (me - distance >= 0) & (me - distance < count)
        self.copy = remote(src, dst, send, recv, jnp.clip(me + distance, 0, count - 1), subs)

    def start(self):
        @pl.when(self.sends)
        def _():
            self.copy.start()

    def wait(self):
        @pl.when(self.sends)
        def _():
            self.copy.wait_send()

        @pl.when(self.gets)
        def _():
            self.copy.wait_recv()


def window_masks(hops, rows, me):
    margin = hops * rows
    row = iota((2 * rows, rows), 0) % rows
    masks = []
    for b in range(hops + 1):
        least, most = margin - (b + 1) * rows + 1, margin + rows - 1 - b * rows
        gap = margin - b * rows + row - iota((2 * rows, rows), 1)
        mask = jnp.broadcast_to(me - (hops - b), gap.shape) >= 0
        if least < 0:
            mask = mask & (gap >= 0)
        if most >= WINDOW:
            mask = mask & (gap < WINDOW)
        masks.append(mask)
    return masks


def causal(keys, queries):
    return keys <= queries


class Coarse:
    def __init__(self, total, span, base, cw, cow, scratch):
        self.total, self.span, self.base = total, span, base
        self.cw, self.cow = cw, cow
        self.uq, self.fq, self.uk, self.fk, self.v, self.g = scratch
        self.width = cw.shape[2]

    def grads(self, cg):
        self.gb = dot_nt(cg, self.cow[...]).astype(BF16)
        self.g[pl.ds(0, self.total), :] = self.gb.astype(F32)

    def project(self, normed):
        uq, fq = head_rms(dot(normed, self.cw[0]))
        uk, fk = head_rms(dot(normed, self.cw[1]))
        v = dot(normed, self.cw[2])
        for ref, value in ((self.uq, uq), (self.fq, fq), (self.uk, uk), (self.fk, fk), (self.v, v)):
            ref[pl.ds(0, self.total), :] = value
        self.qb, self.kb, self.vb = (uq * QUERY).astype(BF16), uk.astype(BF16), v.astype(BF16)

    def sums(self, cols):
        block = min(self.total, 256)
        inverse, deltas = [], []
        for i in range(self.total // block):
            part = slice(i * block, (i + 1) * block)
            q, g = self.qb[part, cols], self.gb[part, cols]
            t, d = [0.0, 0.0], [0.0, 0.0]
            for j in range(i + 1):
                rows = slice(j * block, (j + 1) * block)
                e = jnp.exp2(dot_nt(both(self.kb[rows, cols]), q))
                if j == i:
                    e = jnp.where(causal(iota(e.shape, 0) % block, iota(e.shape, 1)), e, 0.0)
                ed = e * dot_nt(both(self.vb[rows, cols]), g)
                for h in range(2):
                    half = slice(h * block, (h + 1) * block)
                    t[h] = t[h] + jnp.sum(e[half], axis=0, keepdims=True)
                    d[h] = d[h] + jnp.sum(ed[half], axis=0, keepdims=True)
            inverse.append([1.0 / x for x in t])
            deltas.append([x * r for x, r in zip(d, inverse[-1])])
        join = lambda parts, h: jnp.concatenate([x[h] for x in parts], axis=1)
        return [join(inverse, h) for h in range(2)], [join(deltas, h) for h in range(2)]

    def mine(self, ref, cols):
        start = pl.multiple_of(self.base, 8)
        return ref[pl.ds(start, self.span), cols]

    def attend(self):
        span, total = self.span, self.total
        shape = (2 * span, total)
        own = self.base + iota(shape, 0) % span
        after = causal(own, iota(shape, 1))
        before = causal(iota(shape, 1), own)
        att_p, dq_p, dk_p, dv_p = [], [], [], []
        for p in range(self.width // PAIR):
            cols = slice(p * PAIR, (p + 1) * PAIR)
            inverse, deltas = self.sums(cols)
            ds_cols = pl.ds(p * PAIR, PAIR)
            qp, kp, vp, gp = self.qb[:, cols], self.kb[:, cols], self.vb[:, cols], self.gb[:, cols]
            k2, v2 = both(self.mine(self.uk, ds_cols)), both(self.mine(self.v, ds_cols))
            q2, g2 = both(self.mine(self.uq, ds_cols) * QUERY), both(self.mine(self.g, ds_cols))
            wide = lambda pair: jnp.concatenate([jnp.broadcast_to(x, (span, total)) for x in pair])
            pt = jnp.where(after, jnp.exp2(dot_nt(k2, qp)) * wide(inverse), 0.0)
            dst = pt * (dot_nt(v2, gp) - wide(deltas))
            dk_p.append(pick(dot(dst.astype(BF16), qp)) * LN2)
            dv_p.append(pick(dot(pt.astype(BF16), gp)))
            e = jnp.where(before, jnp.exp2(dot_nt(q2, kp)), 0.0)
            e = e * (1.0 / jnp.sum(e, axis=-1, keepdims=True))
            dp = dot_nt(g2, vp)
            delta = jnp.sum(e * dp, axis=-1, keepdims=True)
            ds = e * (dp - delta)
            dq_p.append(pick(dot(ds.astype(BF16), kp)) * SCALE)
            att_p.append(pick(dot(e.astype(BF16), vp)))
        join = lambda parts: jnp.concatenate(parts, axis=1)
        return join(att_p), join(dq_p), join(dk_p), join(dv_p)

    def finish(self, outs_all):
        every = pl.ds(0, self.width)
        att, dq, dk, dv = self.attend()
        mixed = dot(att[:outs_all].astype(BF16), self.cow[...])
        dq = head_back(dq, self.mine(self.uq, every), self.mine(self.fq, every)).astype(BF16)
        dk = head_back(dk, self.mine(self.uk, every), self.mine(self.fk, every)).astype(BF16)
        dv = dv.astype(BF16)
        return mixed, dot_nt(dq, self.cw[0]) + dot_nt(dk, self.cw[1]) + dot_nt(dv, self.cw[2])


def layer_pair(
    hops, x_ref, cot_ref, w_hbm, out_hbm, cw_hbm, cow_hbm, output_ref, grad_ref,
    w_ref, out_w, cw, cow, before, q_all, cot_after, k_all, v_all,
    unit_q, unit_k, scale_q, scale_k, e_ref, t_ref, acc_ref, rt_ref, att_ref, hidden_ref,
    cg_own, cg_all, pool_own, pool_all, pooled, gcot, g_all,
    uq2, fq2, uk2, fk2, v2, g2, mixed_ref, ng_ref, x_out, x_in, stats, stats_after, dq_ref,
    load, halo_sends, halo_recvs, x_sems, stat_sems, *sems,
):
    me, count, subs = place()
    mine, seq = lax.axis_index("sub"), lax.axis_index("seq")
    rows = x_ref.shape[0]
    outs = rows // POOL
    margin, length = hops * rows, (hops + 1) * rows
    total = count * outs
    far = (hops + 2) * outs
    greet_all()
    parts = [
        (w_hbm.at[1], w_ref.at[1]), (w_hbm.at[2], w_ref.at[2]), (w_hbm.at[0], w_ref.at[0]),
        (out_hbm, out_w), (cw_hbm, cw), (cow_hbm, cow),
    ]
    loads = [pltpu.make_async_copy(src, dst, load.at[i]) for i, (src, dst) in enumerate(parts)]
    for one in loads:
        one.start()
    for d in range(1, hops + 1):
        @pl.when(me - d < 0)
        def _():
            before[hops - d] = jnp.zeros((rows, D), BF16)

        @pl.when(me + d >= count)
        def _():
            q_all[d] = jnp.zeros((rows, D), BF16)
            cot_after[d - 1] = jnp.zeros((rows, D), BF16)
            stats_after[d - 1] = jnp.zeros(stats.shape, F32)

    extra = pooled.shape[0] - total
    pooled[pl.ds(total, extra), :] = jnp.zeros((extra, D), F32)
    cg_all[pl.ds(count, extra // outs)] = jnp.zeros((extra // outs, outs, D), BF16)
    for ref in (uq2, fq2, uk2, fk2, v2, g2):
        ref[pl.ds(total, extra), :] = jnp.zeros((extra, ref.shape[1]), F32)
    groups = (iota((outs, rows), 1) // POOL == iota((outs, rows), 0)).astype(F32).astype(BF16)
    cg_own[...] = dot(groups, cot_ref[...]).astype(BF16)
    own = x_ref[...].astype(F32)
    own_b = rms_rows(own)[0].astype(BF16)
    down = Halo(x_ref, before, halo_sends.at[0], halo_recvs.at[0], hops, 1)
    up_cot = Halo(cot_ref, cot_after, halo_sends.at[1], halo_recvs.at[1], hops, -1)
    up = Halo(q_all.at[0], q_all.at[pl.ds(1, hops)], halo_sends.at[2], halo_recvs.at[2], hops, -1)
    cg_spread = Spread(cg_own, cg_all, *sems[:4])
    pool_spread = Spread(pool_own, pool_all, *sems[4:])
    met_all()
    down.start()
    cg_spread.start()
    up_cot.start()
    loads[0].wait()
    unit, factor = head_rms(dot(own_b, w_ref[1]))
    k_all[pl.ds(margin, rows), :] = unit.astype(BF16)
    unit_k[...] = unit
    scale_k[...] = factor
    loads[1].wait()
    v_all[pl.ds(margin, rows), :] = dot(own_b, w_ref[2]).astype(BF16)
    loads[2].wait()
    unit, factor = head_rms(dot(own_b, w_ref[0]))
    q_all[0] = (unit * QUERY).astype(BF16)
    unit_q[...] = unit
    scale_q[...] = factor
    cg_spread.finish()

    def keys(d):
        slot = pl.ds(margin - d * rows, rows)
        prev = rms_rows(before[hops - d].astype(F32))[0].astype(BF16)
        k_all[slot, :] = head_rms(dot(prev, w_ref[1]))[0].astype(BF16)
        v_all[slot, :] = dot(prev, w_ref[2]).astype(BF16)

    masks = window_masks(hops, rows, me)

    def scores(p, low, high):
        cols = pl.ds(p * PAIR, PAIR)
        span = pl.ds(low * rows, (high - low) * rows)
        s = dot_nt(both(q_all[0, :, cols]), k_all[span, cols])
        e = [
            jnp.where(masks[b], jnp.exp2(s[:, (b - low) * rows : (b - low + 1) * rows]), 0.0)
            for b in range(low, high)
        ]
        e_b = jnp.concatenate(e, axis=1).astype(BF16)
        e_ref[p, :, span] = e_b
        return functools.reduce(jnp.add, e), dot(e_b, v_all[span, cols])

    half = hops // 2
    for d in range(1, hops - half + 1):
        down.land(d)
        keys(d)
    for p in range(HEADS // 2):
        t_ref[p], acc_ref[p] = scores(p, half, hops + 1)
    for d in range(hops - half + 1, hops + 1):
        down.land(d)
        keys(d)
    lane = iota((rows, 128), 1)
    totals = jnp.ones((rows, 128), F32)
    for p in range(HEADS // 2):
        t, acc = scores(p, 0, half)
        t = jnp.sum(t + t_ref[p], axis=-1, keepdims=True)
        inverse = jnp.broadcast_to(1.0 / t, (2 * rows, PAIR))
        rt_ref[p] = inverse
        att_ref[:, pl.ds(p * PAIR, PAIR)] = pick((acc + acc_ref[p]) * inverse).astype(BF16)
        totals = jnp.where(lane == 2 * p, t[:rows], totals)
        totals = jnp.where(lane == 2 * p + 1, t[rows:], totals)
    loads[3].wait()
    hidden = (own + dot(att_ref[...], out_w[...])).astype(BF16)
    hidden_ref[...] = hidden
    back = iota((outs, rows), 0) * POOL - iota((outs, rows), 1)
    part = dot(((back >= 0) & (back < POOL)).astype(F32).astype(BF16), hidden)
    tail = dot((iota((outs, rows), 1) > rows - POOL).astype(F32).astype(BF16), hidden)
    lanes = D // outs
    folded = jnp.zeros((outs, lanes), F32)
    for c in range(outs):
        folded = jnp.where(iota((outs, lanes), 0) == c, tail[:, c * lanes : (c + 1) * lanes], folded)
    pool_own[...] = (jnp.concatenate([part, folded], axis=1) / POOL).astype(BF16)
    pool_spread.start()
    up.start()
    up_cot.finish()
    loads[4].wait()
    loads[5].wait()
    base = seq * subs * outs
    span = (subs - 1) * outs + far
    coarse = Coarse(total, span, base, cw, cow, (uq2, fq2, uk2, fk2, v2, g2))
    coarse.grads(cg_all[pl.ds(0, count)].astype(F32).reshape(total, D).astype(BF16))
    gcot[pl.ds(0, rows), :] = dot_nt(cot_ref[...], out_w[...])
    gcot[pl.ds(rows, margin), :] = dot_nt(cot_after[...].reshape(margin, D), out_w[...])
    stats[pl.ds(0, HEADS), :] = jnp.log2(totals.T[:HEADS])
    pool_spread.finish()
    got = pool_all[...].astype(F32).reshape(total, D + lanes)
    block = min(total, 256)
    place_at = (iota((block, block), 0) // outs == iota((block, block), 1) // outs) & (iota((block, block), 0) % outs == 0)
    place_at = place_at.astype(F32).astype(BF16)
    tails = []
    for i in range(total // block):
        one = got[i * block : (i + 1) * block, D:]
        wide = [jnp.where(iota(one.shape, 0) % outs == c, one, 0.0) for c in range(outs)]
        tails.append(dot(place_at, jnp.concatenate(wide, axis=1).astype(BF16)))
    tails = jnp.concatenate([jnp.zeros((outs, D), F32)] + tails)[:total]
    pooled_v = (got[:, :D] + tails).astype(BF16).astype(F32)
    pooled[pl.ds(0, total), :] = pooled_v
    coarse.project(rms_rows(pooled_v)[0].astype(BF16))
    mixed, ng = coarse.finish(subs * outs)
    mixed_ref[...] = mixed
    ng_ref[...] = ng

    def cut(sub):
        start = pl.multiple_of(sub * outs, outs)
        return mixed_ref[pl.ds(start, outs), :], ng_ref[pl.ds(start, far), :]

    copies = []
    for k in range(1, subs):
        other = (mine + k) % subs
        x_out[k] = jnp.concatenate(cut(other)).astype(BF16)
        copies.append(remote(
            x_out.at[k], x_in.at[k], x_sems.at[0, k], x_sems.at[1, k], seq * subs + other, subs
        ))
        copies[-1].start()
    mixed, ng = cut(mine)
    start = pl.multiple_of(me * outs, outs)
    pooled_own = pooled[pl.ds(start, far), :]
    cg = cg_all[pl.ds(me, far // outs)].astype(F32).reshape(far, D)
    normed, factor = rms_rows(pooled_own)
    for copy in copies:
        copy.wait()
    for k in range(1, subs):
        other = x_in[k].astype(F32)
        mixed, ng = mixed + other[:outs], ng + other[outs:]
    pg = (cg + row_back(ng, normed, factor)) / POOL
    pg = jnp.where(me * outs + iota(pg.shape, 0) < total, pg, 0.0).astype(BF16)
    pgw = dot_nt(pg, out_w[...]).astype(BF16)
    lift = ((iota((length, far), 0) + POOL - 1) // POOL == iota((length, far), 1)).astype(F32).astype(BF16)
    g_all[...] = (gcot[...] + dot(lift, pgw)).astype(BF16)
    delta = head_sum(g_all[pl.ds(0, rows), :].astype(F32) * att_ref[...].astype(F32))
    stats[pl.ds(HEADS, HEADS), :] = delta.T[:HEADS]
    moves = [
        Shift(stats, stats_after.at[d - 1], stat_sems.at[0, d - 1], stat_sems.at[1, d - 1], -d)
        for d in range(1, hops + 1)
    ]
    for move in moves:
        move.start()
    up.finish()
    state = (pooled_own[:outs] + mixed).astype(BF16)
    onto = (iota((rows, outs), 0) // POOL == iota((rows, outs), 1)).astype(F32).astype(BF16)
    output_ref[...] = (hidden_ref[...].astype(F32) + dot(onto, state)).astype(BF16)
    for p in range(HEADS // 2):
        cols = pl.ds(p * PAIR, PAIR)
        dp = dot_nt(both(g_all[pl.ds(0, rows), cols]), v_all[:, cols])
        column = jnp.concatenate([delta[:, 2 * p : 2 * p + 1], delta[:, 2 * p + 1 : 2 * p + 2]])
        ds = (e_ref[p].astype(F32) * (dp - column)).astype(BF16)
        dq_ref[:, cols] = pick(dot(ds, k_all[:, cols]) * rt_ref[p]) * SCALE
    for move in moves:
        move.wait()
    gap = iota((rows, length), 1) - iota((rows, length), 0)
    mask_t = (gap >= 0) & (gap < WINDOW)
    every = jnp.concatenate([stats[...]] + [stats_after[d] for d in range(hops)], axis=1)
    dk_p, dv_p = [], []
    for p in range(HEADS // 2):
        cols = pl.ds(p * PAIR, PAIR)
        own_slot = pl.ds(margin, rows)
        qp, gp = q_all[:, :, cols].reshape(length, PAIR), g_all[:, cols]
        st = dot_nt(both(k_all[own_slot, cols]), qp)
        dpt = dot_nt(both(v_all[own_slot, cols]), gp)
        pts, dsts = [], []
        for h in range(2):
            head = 2 * p + h
            part = slice(h * rows, (h + 1) * rows)
            pt = jnp.where(mask_t, jnp.exp2(st[part] - every[head : head + 1]), 0.0)
            pts.append(pt.astype(BF16))
            dsts.append((pt * (dpt[part] - every[HEADS + head : HEADS + head + 1])).astype(BF16))
        dk_p.append(pick(dot(jnp.concatenate(dsts), qp)) * LN2)
        dv_p.append(pick(dot(jnp.concatenate(pts), gp)))
    join = lambda parts: jnp.concatenate(parts, axis=1)
    dq = head_back(dq_ref[...], unit_q[...], scale_q[...]).astype(BF16)
    dk = head_back(join(dk_p), unit_k[...], scale_k[...]).astype(BF16)
    dv = join(dv_p).astype(BF16)
    grads = dot_nt(dq, w_ref[0]) + dot_nt(dk, w_ref[1]) + dot_nt(dv, w_ref[2])
    normed, factor = rms_rows(x_ref[...].astype(F32))
    hidden_grad = cot_ref[...].astype(F32) + dot(lift[:rows], pg)
    grad_ref[...] = (hidden_grad + row_back(grads, normed, factor)).astype(BF16)
    down.drain()
    up_cot.drain()
    up.drain()


def per_device(tokens, cotangent, fine_qkv, fine_out, coarse_qkv, coarse_out):
    rows = tokens.shape[0]
    hops = -(-WINDOW // rows)
    outs = rows // POOL
    me, count, subs = place()
    far = (hops + 2) * outs
    length = (hops + 1) * rows
    total = count * outs
    span = (subs - 1) * outs + far
    width = coarse_qkv.shape[2]
    pairs = HEADS // 2
    shape = jax.ShapeDtypeStruct
    dma = pltpu.SemaphoreType.DMA
    vmem = pltpu.VMEM
    fine_w = jnp.transpose(fine_qkv, (1, 0, 2))
    coarse_w = jnp.transpose(coarse_qkv, (1, 0, 2))
    wide = D + D // outs
    padded = total + far
    scratch = [
        vmem(fine_w.shape, BF16), vmem(fine_out.shape, BF16), vmem(coarse_w.shape, BF16),
        vmem(coarse_out.shape, BF16),
        vmem((hops, rows, D), BF16), vmem((hops + 1, rows, D), BF16), vmem((hops, rows, D), BF16),
        vmem((length, D), BF16), vmem((length, D), BF16),
        vmem((rows, D), F32), vmem((rows, D), F32), vmem((rows, D), F32), vmem((rows, D), F32),
        vmem((pairs, 2 * rows, length), BF16), vmem((pairs, 2 * rows, rows), F32),
        vmem((pairs, 2 * rows, PAIR), F32), vmem((pairs, 2 * rows, PAIR), F32),
        vmem((rows, D), BF16), vmem((rows, D), BF16),
        vmem((outs, D), BF16), vmem((count + far // outs, outs, D), BF16),
        vmem((outs, wide), BF16), vmem((count, outs, wide), BF16),
        vmem((padded, D), F32), vmem((length, D), F32), vmem((length, D), BF16),
    ] + [vmem((padded, width), F32)] * 6 + [
        vmem((subs * outs, D), F32), vmem((span, D), F32),
        vmem((subs, outs + far, D), BF16), vmem((subs, outs + far, D), BF16),
        vmem((2 * HEADS, rows), F32), vmem((hops, 2 * HEADS, rows), F32), vmem((rows, D), F32),
        dma((6,)), dma((3, 2 * hops)), dma((3, hops)), dma((2, subs)), dma((2, hops)),
    ] + spread_sems(count, subs) * 2
    return pl.pallas_call(
        functools.partial(layer_pair, hops),
        out_shape=[shape((rows, D), BF16)] * 2,
        in_specs=[VMEM] * 2 + [ANY] * 4,
        out_specs=[VMEM] * 2,
        scratch_shapes=scratch,
        compiler_params=pltpu.CompilerParams(
            collective_id=0, has_side_effects=True, vmem_limit_bytes=67043328
        ),
    )(tokens, cotangent, fine_w, fine_out, coarse_w, coarse_out)


def solution(mesh):
    placed = (
        P(("seq", "sub"), None),
        P(("seq", "sub"), None),
        P(),
        P(),
        P(None, None, "sub"),
        P("sub", None),
    )
    return jax.shard_map(
        per_device,
        mesh=mesh,
        in_specs=placed,
        out_specs=(P(("seq", "sub"), None), P(("seq", "sub"), None)),
        check_vma=False,
    )
```

time: 132 us -> 85.4 us (0.65)
  the two profiles are of different devices: /device:TPU:3 before, /device:TPU:1 now
where the time goes in v1:
time: 85.4 us; the launch traced here: 85.2 us
  Pallas kernels  81.2 us (95%)
  local copies, waits for them, and re-layouts  3.34 us (4%)
    pallas_call x1, Pallas kernels, per_device(): pl.pallas_call(functools.partial(layer_pair, hops), out_shape=[shape((row...  81.2 us
    unnamed x2, local copies, waits for them, and re-layouts  3.34 us

profile of v1, /device:TPU:1, one launch (start us, length us, event | category | flops | bytes accessed | tf_op | source)
XLA Modules:
  0.0 85.2 jit_solution(9399860761972836427)
XLA Ops:
  0.6 81.2 %shard_map.77 = (bf16[128,1024]{1,0:T(8,128)(2,1)}, bf16[128,1024]{1,0:T(8,128)(2,1)}) custom-call(bf16[128,1024]{1,0:T(8,128)(2,1)} %x_ref.1, bf16[128,1024]{1,0:T(8,128)(2,1)} %cot_ref.1, bf16[3,1024,1024]{2,1,0:T(8,128)(2,1)} %bitcast.2, bf16[1024,1024]{1,0:T(8,128)(2,1)} %out_hbm.1, bf16[3,1024,512]{2,1,0:T(8,128)(2,1)} %bitcast.3, bf16[512,1024]{1,0:T(8,128)(2,1)} %cow_hbm.1), custom_call_target="tpu_custom_call" | custom-call | tf_op jit(solution)/shard_map/pallas_call | solution.py:671
  81.8 1.7 %copy.10 = bf16[128,1024]{1,0:T(8,128)(2,1)} copy(bf16[128,1024]{1,0:T(8,128)(2,1)} %get-tuple-element.4) | data formatting | bytes 524288
  83.5 1.7 %copy.11 = bf16[128,1024]{1,0:T(8,128)(2,1)} copy(bf16[128,1024]{1,0:T(8,128)(2,1)} %get-tuple-element.5) | data formatting | bytes 524288

commit v2 on v1

--- a/solution.py
+++ b/solution.py
@@ -22,7 +22,7 @@
 LN2 = math.log(2.0)
 QUERY = SCALE / LN2
 VMEM = pl.BlockSpec(memory_space=pltpu.VMEM)
-ANY = pl.BlockSpec(memory_space=pl.ANY)
+HBM = pl.BlockSpec(memory_space=pltpu.HBM)
 SMEM = pl.BlockSpec(memory_space=pltpu.SMEM)
 
 
@@ -176,12 +176,13 @@
 
         self.relay(0)
 
-    def finish(self):
+    def widen(self):
         @pl.loop(1, self.groups)
         def _(k):
             self.arrive(0, 0, k).wait_recv()
             self.relay(k)
 
+    def cross(self):
         @pl.loop(0, self.groups)
         def _(k):
             for j in range(1, self.subs):
@@ -189,6 +190,7 @@
                 if self.cores > 1:
                     self.copy(2, j, k).start()
 
+    def finish(self):
         @pl.loop(0, self.groups)
         def _(k):
             for j in range(self.subs):
@@ -408,7 +410,8 @@
 
 
 def layer_pair(
-    hops, x_ref, cot_ref, w_hbm, out_hbm, cw_hbm, cow_hbm, output_ref, grad_ref,
+    hops, x_hbm, cot_hbm, w_hbm, out_hbm, cw_hbm, cow_hbm, output_ref, grad_ref,
+    x_ref, cot_ref,
     w_ref, out_w, cw, cow, before, q_all, cot_after, k_all, v_all,
     unit_q, unit_k, scale_q, scale_k, e_ref, t_ref, acc_ref, rt_ref, att_ref, hidden_ref,
     cg_own, cg_all, pool_own, pool_all, pooled, gcot, g_all,
@@ -425,10 +428,10 @@
     greet_all()
     parts = [
         (w_hbm.at[1], w_ref.at[1]), (w_hbm.at[2], w_ref.at[2]), (w_hbm.at[0], w_ref.at[0]),
-        (out_hbm, out_w), (cw_hbm, cw), (cow_hbm, cow),
+        (out_hbm, out_w), (cw_hbm, cw), (cow_hbm, cow), (x_hbm, x_ref), (cot_hbm, cot_ref),
     ]
     loads = [pltpu.make_async_copy(src, dst, load.at[i]) for i, (src, dst) in enumerate(parts)]
-    for one in loads:
+    for one in loads[6:] + loads[:6]:
         one.start()
     for d in range(1, hops + 1):
         @pl.when(me - d < 0)
@@ -446,6 +449,8 @@
     cg_all[pl.ds(count, extra // outs)] = jnp.zeros((extra // outs, outs, D), BF16)
     for ref in (uq2, fq2, uk2, fk2, v2, g2):
         ref[pl.ds(total, extra), :] = jnp.zeros((extra, ref.shape[1]), F32)
+    loads[6].wait()
+    loads[7].wait()
     groups = (iota((outs, rows), 1) // POOL == iota((outs, rows), 0)).astype(F32).astype(BF16)
     cg_own[...] = dot(groups, cot_ref[...]).astype(BF16)
     own = x_ref[...].astype(F32)
@@ -471,7 +476,6 @@
     q_all[0] = (unit * QUERY).astype(BF16)
     unit_q[...] = unit
     scale_q[...] = factor
-    cg_spread.finish()
 
     def keys(d):
         slot = pl.ds(margin - d * rows, rows)
@@ -497,11 +501,13 @@
     for d in range(1, hops - half + 1):
         down.land(d)
         keys(d)
+    cg_spread.widen()
     for p in range(HEADS // 2):
         t_ref[p], acc_ref[p] = scores(p, half, hops + 1)
     for d in range(hops - half + 1, hops + 1):
         down.land(d)
         keys(d)
+    cg_spread.cross()
     lane = iota((rows, 128), 1)
     totals = jnp.ones((rows, 128), F32)
     for p in range(HEADS // 2):
@@ -524,7 +530,7 @@
         folded = jnp.where(iota((outs, lanes), 0) == c, tail[:, c * lanes : (c + 1) * lanes], folded)
     pool_own[...] = (jnp.concatenate([part, folded], axis=1) / POOL).astype(BF16)
     pool_spread.start()
-    up.start()
+    cg_spread.finish()
     up_cot.finish()
     loads[4].wait()
     loads[5].wait()
@@ -535,7 +541,10 @@
     gcot[pl.ds(0, rows), :] = dot_nt(cot_ref[...], out_w[...])
     gcot[pl.ds(rows, margin), :] = dot_nt(cot_after[...].reshape(margin, D), out_w[...])
     stats[pl.ds(0, HEADS), :] = jnp.log2(totals.T[:HEADS])
+    pool_spread.widen()
+    pool_spread.cross()
     pool_spread.finish()
+    up.start()
     got = pool_all[...].astype(F32).reshape(total, D + lanes)
     block = min(total, 256)
     place_at = (iota((block, block), 0) // outs == iota((block, block), 1) // outs) & (iota((block, block), 0) % outs == 0)
@@ -588,7 +597,6 @@
     ]
     for move in moves:
         move.start()
-    up.finish()
     state = (pooled_own[:outs] + mixed).astype(BF16)
     onto = (iota((rows, outs), 0) // POOL == iota((rows, outs), 1)).astype(F32).astype(BF16)
     output_ref[...] = (hidden_ref[...].astype(F32) + dot(onto, state)).astype(BF16)
@@ -598,6 +606,7 @@
         column = jnp.concatenate([delta[:, 2 * p : 2 * p + 1], delta[:, 2 * p + 1 : 2 * p + 2]])
         ds = (e_ref[p].astype(F32) * (dp - column)).astype(BF16)
         dq_ref[:, cols] = pick(dot(ds, k_all[:, cols]) * rt_ref[p]) * SCALE
+    up.finish()
     for move in moves:
         move.wait()
     gap = iota((rows, length), 1) - iota((rows, length), 0)
@@ -651,6 +660,7 @@
     wide = D + D // outs
     padded = total + far
     scratch = [
+        vmem((rows, D), BF16), vmem((rows, D), BF16),
         vmem(fine_w.shape, BF16), vmem(fine_out.shape, BF16), vmem(coarse_w.shape, BF16),
         vmem(coarse_out.shape, BF16),
         vmem((hops, rows, D), BF16), vmem((hops + 1, rows, D), BF16), vmem((hops, rows, D), BF16),
@@ -666,18 +676,21 @@
         vmem((subs * outs, D), F32), vmem((span, D), F32),
         vmem((subs, outs + far, D), BF16), vmem((subs, outs + far, D), BF16),
         vmem((2 * HEADS, rows), F32), vmem((hops, 2 * HEADS, rows), F32), vmem((rows, D), F32),
-        dma((6,)), dma((3, 2 * hops)), dma((3, hops)), dma((2, subs)), dma((2, hops)),
+        dma((8,)), dma((3, 2 * hops)), dma((3, hops)), dma((2, subs)), dma((2, hops)),
     ] + spread_sems(count, subs) * 2
     return pl.pallas_call(
         functools.partial(layer_pair, hops),
         out_shape=[shape((rows, D), BF16)] * 2,
-        in_specs=[VMEM] * 2 + [ANY] * 4,
+        in_specs=[HBM] * 6,
         out_specs=[VMEM] * 2,
         scratch_shapes=scratch,
         compiler_params=pltpu.CompilerParams(
-            collective_id=0, has_side_effects=True, vmem_limit_bytes=67043328
+            collective_id=0, has_side_effects=True, vmem_limit_bytes=(48 if total <= 1024 else 63) * 1024 * 1024
         ),
-    )(tokens, cotangent, fine_w, fine_out, coarse_w, coarse_out)
+    )(*[
+        pltpu.with_memory_space_constraint(a, pltpu.HBM)
+        for a in (tokens, cotangent, fine_w, fine_out, coarse_w, coarse_out)
+    ])
 
 
 def solution(mesh):

time: 85.4 us -> 72.7 us (0.85)
  the two profiles are of different devices: /device:TPU:1 before, /device:TPU:12 now
where the time goes in v2:
time: 72.7 us; the launch traced here: 72.6 us
  Pallas kernels  70.5 us (97%)
  local copies, waits for them, and re-layouts  1.41 us (2%)
    pallas_call x1, Pallas kernels, per_device(): pl.pallas_call(functools.partial(layer_pair, hops), out_shape=[shape((row...  70.5 us

profile of v2, /device:TPU:12, one launch (start us, length us, event | category | flops | bytes accessed | tf_op | source)
XLA Modules:
  0.0 72.6 jit_solution(925556818368255205)
XLA Ops:
  0.6 70.5 %shard_map.77 = (bf16[128,1024]{1,0:T(8,128)(2,1)S(1)}, bf16[128,1024]{1,0:T(8,128)(2,1)S(1)}) custom-call(bf16[128,1024]{1,0:T(8,128)(2,1)} %x_hbm.1, bf16[128,1024]{1,0:T(8,128)(2,1)} %cot_hbm.1, bf16[3,1024,1024]{2,1,0:T(8,128)(2,1)} %bitcast.2, bf16[1024,1024]{1,0:T(8,128)(2,1)} %out_hbm.1, bf16[3,1024,512]{2,1,0:T(8,128)(2,1)} %bitcast.3, ...), custom_call_target="tpu_custom_call" | custom-call | tf_op jit(solution)/shard_map/pallas_call | solution.py:681
  71.1 0.7 copy.10
  71.8 0.7 copy.11

commit v3 on v2

--- a/solution.py
+++ b/solution.py
@@ -13,6 +13,7 @@
 HEAD_DIM = 64
 WINDOW = 512
 POOL = 16
+PIECES = 4
 EPS = 1e-06
 F32 = jnp.float32
 BF16 = jnp.bfloat16
@@ -255,7 +256,11 @@
             def _():
                 self.direct(d).start()
 
-    def land(self, d):
+    def land(self, *near):
+        for d in near:
+            self.land_one(d)
+
+    def land_one(self, d):
         @pl.when(self.inside(self.me - self.sign * d))
         def _():
             self.direct(d).wait_recv()
@@ -265,9 +270,9 @@
             def _():
                 self.passed(d).start()
 
-    def finish(self):
-        for d in range(1, self.hops + 1):
-            self.land(d)
+    def stage(self, number):
+        if number == 0:
+            self.land(*range(1, self.hops + 1))
 
     def drain(self):
         for d in range(1, self.hops + 1):
@@ -279,6 +284,94 @@
                 @pl.when(self.relays(d))
                 def _():
                     self.passed(d).wait_send()
+
+
+class Braid:
+    def __init__(self, src, dst, sends, recvs, hops, sign):
+        self.me, self.count, self.subs = place()
+        self.src, self.dst, self.sends, self.recvs = src, dst, sends, recvs
+        self.hops, self.sign = hops, sign
+        self.rank = self.me if sign > 0 else self.count - 1 - self.me
+        self.side, self.core = self.rank % 2, self.rank // 2 % 2
+        self.size = src.shape[0] // PIECES
+
+    def slot(self, d):
+        return self.dst.at[self.hops - d if self.sign > 0 else d - 1]
+
+    def copy(self, kind, source, d, to, slot, piece):
+        span = pl.ds(piece * self.size, self.size)
+        target = jnp.clip(self.me + self.sign * to, 0, self.count - 1)
+        return remote(
+            source.at[span], self.slot(slot).at[span], self.sends.at[kind, d - 1, piece],
+            self.recvs.at[slot - 1, piece], target, self.subs,
+        )
+
+    def direct(self, d, piece):
+        return self.copy(0, self.src, d, d, d, piece)
+
+    def across(self, d, piece):
+        step = 1 - 2 * self.side
+        return self.copy(1, self.slot(d), d, step, d + step, piece)
+
+    def passed(self, d, piece):
+        return self.copy(2, self.slot(d), d, 2, d + 2, piece)
+
+    def routes(self):
+        near = self.core == 0
+        return [
+            (self.direct, 2, self.rank + 2 < self.count),
+            (self.direct, 4, near & (self.rank + 4 < self.count)),
+            (self.direct, 1, (self.rank % 4 != 3) & (self.rank + 1 < self.count)),
+            (self.across, 2, near & (self.rank >= 2)),
+            (self.across, 4, near & (self.side == 1) & (self.rank >= 4)),
+            (self.passed, 1, near & (self.rank >= 1)),
+            (self.passed, 2, near & (self.rank >= 2)),
+        ]
+
+    def start(self):
+        for make, d, used in self.routes()[:3]:
+            @pl.when(used)
+            def _():
+                for piece in range(PIECES):
+                    make(d, piece).start()
+
+    def land(self, *near):
+        for piece in range(PIECES):
+            for d in near:
+                @pl.when(self.rank >= d)
+                def _():
+                    self.direct(d, piece).wait_recv()
+
+                for make, other, used in self.routes()[3:]:
+                    if other == d:
+                        @pl.when(used)
+                        def _():
+                            make(d, piece).start()
+
+    def stage(self, number):
+        self.land(*((2, 4), (1,), (3,))[number])
+
+    def drain(self):
+        for make, d, used in self.routes():
+            @pl.when(used)
+            def _():
+                for piece in range(PIECES):
+                    make(d, piece).wait_send()
+
+
+def braided(hops):
+    return lax.axis_size("sub") == 2 and lax.axis_size("seq") % 2 == 0 and hops == 4
+
+
+def halo(hops, *args):
+    return (Braid if braided(hops) else Halo)(*args)
+
+
+def halo_sems(hops, number):
+    dma = pltpu.SemaphoreType.DMA
+    if braided(hops):
+        return [dma((number, 3, hops, PIECES)), dma((number, hops, PIECES))]
+    return [dma((number, 2 * hops)), dma((number, hops))]
 
 
 class Shift:
@@ -455,9 +548,9 @@
     cg_own[...] = dot(groups, cot_ref[...]).astype(BF16)
     own = x_ref[...].astype(F32)
     own_b = rms_rows(own)[0].astype(BF16)
-    down = Halo(x_ref, before, halo_sends.at[0], halo_recvs.at[0], hops, 1)
-    up_cot = Halo(cot_ref, cot_after, halo_sends.at[1], halo_recvs.at[1], hops, -1)
-    up = Halo(q_all.at[0], q_all.at[pl.ds(1, hops)], halo_sends.at[2], halo_recvs.at[2], hops, -1)
+    down = halo(hops, x_ref, before, halo_sends.at[0], halo_recvs.at[0], hops, 1)
+    up_cot = halo(hops, cot_ref, cot_after, halo_sends.at[1], halo_recvs.at[1], hops, -1)
+    up = halo(hops, q_all.at[0], q_all.at[pl.ds(1, hops)], halo_sends.at[2], halo_recvs.at[2], hops, -1)
     cg_spread = Spread(cg_own, cg_all, *sems[:4])
     pool_spread = Spread(pool_own, pool_all, *sems[4:])
     met_all()
@@ -498,15 +591,31 @@
         return functools.reduce(jnp.add, e), dot(e_b, v_all[span, cols])
 
     half = hops // 2
-    for d in range(1, hops - half + 1):
-        down.land(d)
-        keys(d)
-    cg_spread.widen()
-    for p in range(HEADS // 2):
-        t_ref[p], acc_ref[p] = scores(p, half, hops + 1)
-    for d in range(hops - half + 1, hops + 1):
-        down.land(d)
-        keys(d)
+    if braided(hops):
+        down.land(2, 4)
+        keys(2)
+        keys(4)
+        down.land(1)
+        up_cot.stage(0)
+        keys(1)
+        cg_spread.widen()
+        for p in range(HEADS // 2):
+            t_ref[p], acc_ref[p] = scores(p, half, hops + 1)
+        down.land(3)
+        up_cot.stage(1)
+        keys(3)
+    else:
+        for d in range(1, hops - half + 1):
+            down.land(d)
+            keys(d)
+        cg_spread.widen()
+        for p in range(HEADS // 2):
+            t_ref[p], acc_ref[p] = scores(p, half, hops + 1)
+        for d in range(hops - half + 1, hops + 1):
+            down.land(d)
+            keys(d)
+        up_cot.stage(0)
+        up_cot.stage(1)
     cg_spread.cross()
     lane = iota((rows, 128), 1)
     totals = jnp.ones((rows, 128), F32)
@@ -531,7 +640,7 @@
     pool_own[...] = (jnp.concatenate([part, folded], axis=1) / POOL).astype(BF16)
     pool_spread.start()
     cg_spread.finish()
-    up_cot.finish()
+    up_cot.stage(2)
     loads[4].wait()
     loads[5].wait()
     base = seq * subs * outs
@@ -574,6 +683,7 @@
             x_out.at[k], x_in.at[k], x_sems.at[0, k], x_sems.at[1, k], seq * subs + other, subs
         ))
         copies[-1].start()
+    up.stage(0)
     mixed, ng = cut(mine)
     start = pl.multiple_of(me * outs, outs)
     pooled_own = pooled[pl.ds(start, far), :]
@@ -597,6 +707,7 @@
     ]
     for move in moves:
         move.start()
+    up.stage(1)
     state = (pooled_own[:outs] + mixed).astype(BF16)
     onto = (iota((rows, outs), 0) // POOL == iota((rows, outs), 1)).astype(F32).astype(BF16)
     output_ref[...] = (hidden_ref[...].astype(F32) + dot(onto, state)).astype(BF16)
@@ -606,7 +717,7 @@
         column = jnp.concatenate([delta[:, 2 * p : 2 * p + 1], delta[:, 2 * p + 1 : 2 * p + 2]])
         ds = (e_ref[p].astype(F32) * (dp - column)).astype(BF16)
         dq_ref[:, cols] = pick(dot(ds, k_all[:, cols]) * rt_ref[p]) * SCALE
-    up.finish()
+    up.stage(2)
     for move in moves:
         move.wait()
     gap = iota((rows, length), 1) - iota((rows, length), 0)
@@ -676,7 +787,7 @@
         vmem((subs * outs, D), F32), vmem((span, D), F32),
         vmem((subs, outs + far, D), BF16), vmem((subs, outs + far, D), BF16),
         vmem((2 * HEADS, rows), F32), vmem((hops, 2 * HEADS, rows), F32), vmem((rows, D), F32),
-        dma((8,)), dma((3, 2 * hops)), dma((3, hops)), dma((2, subs)), dma((2, hops)),
+        dma((8,)), *halo_sems(hops, 3), dma((2, subs)), dma((2, hops)),
     ] + spread_sems(count, subs) * 2
     return pl.pallas_call(
         functools.partial(layer_pair, hops),

time: 72.7 us -> 69.7 us (0.959)
  the two profiles are of different devices: /device:TPU:12 before, /device:TPU:3 now
where the time goes in v3:
time: 69.7 us; the launch traced here: 69.5 us
  Pallas kernels  67.5 us (97%)
  local copies, waits for them, and re-layouts  1.41 us (2%)
    pallas_call x1, Pallas kernels, per_device(): pl.pallas_call(functools.partial(layer_pair, hops), out_shape=[shape((row...  67.5 us
    unnamed x2, local copies, waits for them, and re-layouts  1.41 us

profile of v3, /device:TPU:3, one launch (start us, length us, event | category | flops | bytes accessed | tf_op | source)
XLA Modules:
  0.0 69.5 jit_solution(5902207259909528356)
XLA Ops:
  0.6 67.5 %shard_map.77 = (bf16[128,1024]{1,0:T(8,128)(2,1)S(1)}, bf16[128,1024]{1,0:T(8,128)(2,1)S(1)}) custom-call(bf16[128,1024]{1,0:T(8,128)(2,1)} %x_hbm.1, bf16[128,1024]{1,0:T(8,128)(2,1)} %cot_hbm.1, bf16[3,1024,1024]{2,1,0:T(8,128)(2,1)} %bitcast.2, bf16[1024,1024]{1,0:T(8,128)(2,1)} %out_hbm.1, bf16[3,1024,512]{2,1,0:T(8,128)(2,1)} %bitcast.3, ...), custom_call_target="tpu_custom_call" | custom-call | tf_op jit(solution)/shard_map/pallas_call | solution.py:792
  68.1 0.7 %copy.10 = bf16[128,1024]{1,0:T(8,128)(2,1)} copy(bf16[128,1024]{1,0:T(8,128)(2,1)S(1)} %get-tuple-element.4) | data formatting | bytes 524288
  68.8 0.7 %copy.11 = bf16[128,1024]{1,0:T(8,128)(2,1)} copy(bf16[128,1024]{1,0:T(8,128)(2,1)S(1)} %get-tuple-element.5) | data formatting | bytes 524288

commit v4 on v3

--- a/solution.py
+++ b/solution.py
@@ -556,7 +556,6 @@
     met_all()
     down.start()
     cg_spread.start()
-    up_cot.start()
     loads[0].wait()
     unit, factor = head_rms(dot(own_b, w_ref[1]))
     k_all[pl.ds(margin, rows), :] = unit.astype(BF16)
@@ -578,7 +577,8 @@
 
     masks = window_masks(hops, rows, me)
 
-    def scores(p, low, high):
+    def scores(p, blocks):
+        low, high = blocks[0], blocks[-1] + 1
         cols = pl.ds(p * PAIR, PAIR)
         span = pl.ds(low * rows, (high - low) * rows)
         s = dot_nt(both(q_all[0, :, cols]), k_all[span, cols])
@@ -592,35 +592,35 @@
 
     half = hops // 2
     if braided(hops):
+        for p in range(HEADS // 2):
+            t_ref[p], acc_ref[p] = scores(p, [hops])
         down.land(2, 4)
         keys(2)
         keys(4)
         down.land(1)
-        up_cot.stage(0)
         keys(1)
         cg_spread.widen()
-        for p in range(HEADS // 2):
-            t_ref[p], acc_ref[p] = scores(p, half, hops + 1)
         down.land(3)
-        up_cot.stage(1)
+        up_cot.start()
         keys(3)
+        late = range(0, hops)
     else:
         for d in range(1, hops - half + 1):
             down.land(d)
             keys(d)
         cg_spread.widen()
         for p in range(HEADS // 2):
-            t_ref[p], acc_ref[p] = scores(p, half, hops + 1)
+            t_ref[p], acc_ref[p] = scores(p, range(half, hops + 1))
         for d in range(hops - half + 1, hops + 1):
             down.land(d)
             keys(d)
-        up_cot.stage(0)
-        up_cot.stage(1)
+        late = range(0, half)
+        up_cot.start()
     cg_spread.cross()
     lane = iota((rows, 128), 1)
     totals = jnp.ones((rows, 128), F32)
     for p in range(HEADS // 2):
-        t, acc = scores(p, 0, half)
+        t, acc = scores(p, late)
         t = jnp.sum(t + t_ref[p], axis=-1, keepdims=True)
         inverse = jnp.broadcast_to(1.0 / t, (2 * rows, PAIR))
         rt_ref[p] = inverse
@@ -640,19 +640,18 @@
     pool_own[...] = (jnp.concatenate([part, folded], axis=1) / POOL).astype(BF16)
     pool_spread.start()
     cg_spread.finish()
-    up_cot.stage(2)
     loads[4].wait()
     loads[5].wait()
     base = seq * subs * outs
     span = (subs - 1) * outs + far
     coarse = Coarse(total, span, base, cw, cow, (uq2, fq2, uk2, fk2, v2, g2))
     coarse.grads(cg_all[pl.ds(0, count)].astype(F32).reshape(total, D).astype(BF16))
-    gcot[pl.ds(0, rows), :] = dot_nt(cot_ref[...], out_w[...])
-    gcot[pl.ds(rows, margin), :] = dot_nt(cot_after[...].reshape(margin, D), out_w[...])
+    gcot[...] = dot_nt(cot_ref[...], out_w[...])
     stats[pl.ds(0, HEADS), :] = jnp.log2(totals.T[:HEADS])
     pool_spread.widen()
     pool_spread.cross()
     pool_spread.finish()
+    up_cot.stage(0)
     up.start()
     got = pool_all[...].astype(F32).reshape(total, D + lanes)
     block = min(total, 256)
@@ -683,6 +682,7 @@
             x_out.at[k], x_in.at[k], x_sems.at[0, k], x_sems.at[1, k], seq * subs + other, subs
         ))
         copies[-1].start()
+    up_cot.stage(1)
     up.stage(0)
     mixed, ng = cut(mine)
     start = pl.multiple_of(me * outs, outs)
@@ -698,7 +698,7 @@
     pg = jnp.where(me * outs + iota(pg.shape, 0) < total, pg, 0.0).astype(BF16)
     pgw = dot_nt(pg, out_w[...]).astype(BF16)
     lift = ((iota((length, far), 0) + POOL - 1) // POOL == iota((length, far), 1)).astype(F32).astype(BF16)
-    g_all[...] = (gcot[...] + dot(lift, pgw)).astype(BF16)
+    g_all[pl.ds(0, rows), :] = (gcot[...] + dot(lift[:rows], pgw)).astype(BF16)
     delta = head_sum(g_all[pl.ds(0, rows), :].astype(F32) * att_ref[...].astype(F32))
     stats[pl.ds(HEADS, HEADS), :] = delta.T[:HEADS]
     moves = [
@@ -717,6 +717,11 @@
         column = jnp.concatenate([delta[:, 2 * p : 2 * p + 1], delta[:, 2 * p + 1 : 2 * p + 2]])
         ds = (e_ref[p].astype(F32) * (dp - column)).astype(BF16)
         dq_ref[:, cols] = pick(dot(ds, k_all[:, cols]) * rt_ref[p]) * SCALE
+    dq = head_back(dq_ref[...], unit_q[...], scale_q[...]).astype(BF16)
+    dq_ref[...] = dot_nt(dq, w_ref[0])
+    up_cot.stage(2)
+    later = dot_nt(cot_after[...].reshape(margin, D), out_w[...])
+    g_all[pl.ds(rows, margin), :] = (later + dot(lift[rows:], pgw)).astype(BF16)
     up.stage(2)
     for move in moves:
         move.wait()
@@ -740,10 +745,9 @@
         dk_p.append(pick(dot(jnp.concatenate(dsts), qp)) * LN2)
         dv_p.append(pick(dot(jnp.concatenate(pts), gp)))
     join = lambda parts: jnp.concatenate(parts, axis=1)
-    dq = head_back(dq_ref[...], unit_q[...], scale_q[...]).astype(BF16)
     dk = head_back(join(dk_p), unit_k[...], scale_k[...]).astype(BF16)
     dv = join(dv_p).astype(BF16)
-    grads = dot_nt(dq, w_ref[0]) + dot_nt(dk, w_ref[1]) + dot_nt(dv, w_ref[2])
+    grads = dq_ref[...] + dot_nt(dk, w_ref[1]) + dot_nt(dv, w_ref[2])
     normed, factor = rms_rows(x_ref[...].astype(F32))
     hidden_grad = cot_ref[...].astype(F32) + dot(lift[:rows], pg)
     grad_ref[...] = (hidden_grad + row_back(grads, normed, factor)).astype(BF16)
@@ -782,7 +786,7 @@
         vmem((rows, D), BF16), vmem((rows, D), BF16),
         vmem((outs, D), BF16), vmem((count + far // outs, outs, D), BF16),
         vmem((outs, wide), BF16), vmem((count, outs, wide), BF16),
-        vmem((padded, D), F32), vmem((length, D), F32), vmem((length, D), BF16),
+        vmem((padded, D), F32), vmem((rows, D), F32), vmem((length, D), BF16),
     ] + [vmem((padded, width), F32)] * 6 + [
         vmem((subs * outs, D), F32), vmem((span, D), F32),
         vmem((subs, outs + far, D), BF16), vmem((subs, outs + far, D), BF16),

time: 69.7 us -> 67.3 us (0.966)
  Pallas kernels: 67.5 us -> 65.1 us
    pallas_call x1, Pallas kernels: 67.5 us -> 65.1 us  [per_device(): pl.pallas_call(functools.partial(layer_pair, hops), out_shape=[shape((row...]
where the time goes in v4:
time: 67.3 us; the launch traced here: 67.1 us
  Pallas kernels  65.1 us (97%)
  local copies, waits for them, and re-layouts  1.41 us (2%)
    pallas_call x1, Pallas kernels, per_device(): pl.pallas_call(functools.partial(layer_pair, hops), out_shape=[shape((row...  65.1 us
    unnamed x2, local copies, waits for them, and re-layouts  1.41 us

profile of v4, /device:TPU:3, one launch (start us, length us, event | category | flops | bytes accessed | tf_op | source)
XLA Modules:
  0.0 67.1 jit_solution(16197492418728066871)
XLA Ops:
  0.6 65.1 %shard_map.77 = (bf16[128,1024]{1,0:T(8,128)(2,1)S(1)}, bf16[128,1024]{1,0:T(8,128)(2,1)S(1)}) custom-call(bf16[128,1024]{1,0:T(8,128)(2,1)} %x_hbm.1, bf16[128,1024]{1,0:T(8,128)(2,1)} %cot_hbm.1, bf16[3,1024,1024]{2,1,0:T(8,128)(2,1)} %bitcast.2, bf16[1024,1024]{1,0:T(8,128)(2,1)} %out_hbm.1, bf16[3,1024,512]{2,1,0:T(8,128)(2,1)} %bitcast.3, ...), custom_call_target="tpu_custom_call" | custom-call | tf_op jit(solution)/shard_map/pallas_call | solution.py:796
  65.7 0.7 %copy.10 = bf16[128,1024]{1,0:T(8,128)(2,1)} copy(bf16[128,1024]{1,0:T(8,128)(2,1)S(1)} %get-tuple-element.4) | data formatting | bytes 524288
  66.4 0.7 %copy.11 = bf16[128,1024]{1,0:T(8,128)(2,1)} copy(bf16[128,1024]{1,0:T(8,128)(2,1)S(1)} %get-tuple-element.5) | data formatting | bytes 524288

commit v5 on v4

--- a/solution.py
+++ b/solution.py
@@ -13,7 +13,7 @@
 HEAD_DIM = 64
 WINDOW = 512
 POOL = 16
-PIECES = 4
+PIECES = 2
 EPS = 1e-06
 F32 = jnp.float32
 BF16 = jnp.bfloat16

time: 67.3 us -> 66 us (0.981)
  Pallas kernels: 65.1 us -> 63.8 us
    pallas_call x1, Pallas kernels: 65.1 us -> 63.8 us  [per_device(): pl.pallas_call(functools.partial(layer_pair, hops), out_shape=[shape((row...]
where the time goes in v5:
time: 66 us; the launch traced here: 65.9 us
  Pallas kernels  63.8 us (97%)
  local copies, waits for them, and re-layouts  1.41 us (2%)
    pallas_call x1, Pallas kernels, per_device(): pl.pallas_call(functools.partial(layer_pair, hops), out_shape=[shape((row...  63.8 us
    unnamed x2, local copies, waits for them, and re-layouts  1.41 us

profile of v5, /device:TPU:3, one launch (start us, length us, event | category | flops | bytes accessed | tf_op | source)
XLA Modules:
  0.0 65.9 jit_solution(13429558533440156730)
XLA Ops:
  0.6 63.8 %shard_map.77 = (bf16[128,1024]{1,0:T(8,128)(2,1)S(1)}, bf16[128,1024]{1,0:T(8,128)(2,1)S(1)}) custom-call(bf16[128,1024]{1,0:T(8,128)(2,1)} %x_hbm.1, bf16[128,1024]{1,0:T(8,128)(2,1)} %cot_hbm.1, bf16[3,1024,1024]{2,1,0:T(8,128)(2,1)} %bitcast.2, bf16[1024,1024]{1,0:T(8,128)(2,1)} %out_hbm.1, bf16[3,1024,512]{2,1,0:T(8,128)(2,1)} %bitcast.3, ...), custom_call_target="tpu_custom_call" | custom-call | tf_op jit(solution)/shard_map/pallas_call | solution.py:796
  64.5 0.7 %copy.10 = bf16[128,1024]{1,0:T(8,128)(2,1)} copy(bf16[128,1024]{1,0:T(8,128)(2,1)S(1)} %get-tuple-element.4) | data formatting | bytes 524288
  65.2 0.7 %copy.11 = bf16[128,1024]{1,0:T(8,128)(2,1)} copy(bf16[128,1024]{1,0:T(8,128)(2,1)S(1)} %get-tuple-element.5) | data formatting | bytes 524288
